TPU v7x, 32 devices: a whole 2x2x4 slice. The times are simulated.
32 devices in a mesh: agg: 2 (over y), gx: 4 (over x, core), gy: 4 (over z).
Axes of the slice: x: 2, y: 2, z: 4, core: 2. Of those that a mesh axis runs over, the one named last changes fastest.
Arguments:
- velocity_prev: float32 [3, 32, 64, 256], P(None, 'gx', 'gy', 'agg'), may hold values from -6 to 6
- forcing: float32 [3, 32, 64, 256], P(None, 'gx', 'gy', 'agg'), may hold values from -6 to 6
- reaction: float32 [32, 64, 256], P('gx', 'gy', 'agg'), may hold values from 0.1 to 4
Outputs:
- velocity: float32 [3, 32, 64, 256], P(None, 'gx', 'gy', 'agg')
- compressed: float32 [3, 64, 256, 16], P(None, 'gy', ('agg', 'gx'))
All inputs are finite; a program needn't handle non-finite values.
Results may differ from a plain program's by a relative error of at most 0.00002.
Values sent between devices are 32-bit elements; how exact they have to be, the bound alone decides.
A program may use at most 64 MiB of HBM per device.

v0:
```python
import functools

import jax
import jax.numpy as jnp
import numpy as np
from jax import lax
from jax.experimental import pallas as pl
from jax.experimental.pallas import tpu as pltpu
from jax.sharding import PartitionSpec as P

SWEEPS = 2
COARSE_SWEEPS = 4
LX = 5
MESH = pl.DeviceIdType.MESH

damping = 0.8
keep = 1.0 - damping
root_half = 0.7071067811865476


def local_levels(cells_x):
    return min(LX, cells_x.bit_length() - 1)


def finish_matrix(cells_x, blocks, rows):
    levels = local_levels(cells_x)
    kept = cells_x // 2
    eye = np.eye(blocks * kept).reshape(blocks, kept, blocks * kept)
    width = cells_x >> levels
    approx = eye[:, :width].reshape(blocks * width, -1)
    details, at = [], width
    for level in range(levels, 1, -1):
        width = cells_x >> level
        details.append(eye[:, at : at + width].reshape(blocks * width, -1))
        at += width
    for level in range(levels, LX):
        low, high = approx[0::2], approx[1::2]
        approx, detail = (low + high) * root_half, (low - high) * root_half
        details.insert(0, detail)
    along_x = np.concatenate([approx] + details, axis=0)
    along_y = np.zeros((rows, rows))
    for row in range(0, rows, 2):
        along_y[row, row : row + 2] = root_half
        along_y[row + 1, row : row + 2] = root_half, -root_half
    return np.einsum("qk,yr->yqkr", along_x, along_y).reshape(-1, blocks * kept * rows).astype(np.float32)


def neighbour_sides():
    return [(axis, high) for axis in ("gx", "gy", "agg") for high in (False, True)]


def edge_sides():
    pairs = (("gx", "gy"), ("gx", "agg"), ("gy", "agg"))
    return [((a, p), (b, q)) for a, b in pairs for p in (False, True) for q in (False, True)]


def kernel(
    sizes, v_hbm, f_hbm, r_hbm, m_hbm, vel_ref, comp_ref, v_ref, f_ref, r_ref, m_ref,
    xs_fine, xr_fine, ys_fine, yr_fine, zs_fine, zr_fine,
    xs_coarse, xr_coarse, ys_coarse, yr_coarse, zs_coarse, zr_coarse,
    xs_deep, xr_deep, ys_deep, yr_deep, zs_deep, zr_deep, exy, exz, eyz,
c_send, c_recv, w_buf, send_sem, recv_sem, deep_send_sem, deep_recv_sem, c_send_sem, c_recv_sem, in_sem,
):
    counts = sizes
    C, X, Y, Z = v_ref.shape
    Xc = X // 2
    half = Z // 2
    me = {axis: lax.axis_index(axis) for axis in counts}
    blocks = counts["gx"]
    chunk = Z // blocks

    def exists(axis, high):
        return me[axis] < counts[axis] - 1 if high else me[axis] > 0

    loads = [
        pltpu.make_async_copy(src, dst, in_sem.at[i])
        for i, (src, dst) in enumerate(
            ((v_hbm, v_ref), (f_hbm, f_ref), (r_hbm, r_ref), (m_hbm, m_ref))
        )
    ]
    for load in loads:
        load.start()
    def beside(*sides):
        return {axis: me[axis] + (1 if high else -1) for axis, high in sides}

    barrier = pltpu.get_barrier_semaphore()
    expected = blocks - 1
    for step in range(1, blocks):
        pl.semaphore_signal(
            barrier, inc=1, device_id={"gx": lax.rem(me["gx"] + step, blocks)}, device_id_type=MESH
        )
    for axis, high in neighbour_sides()[2:]:
        there = exists(axis, high)
        expected = expected + there.astype(jnp.int32)

        @pl.when(there)
        def _():
            pl.semaphore_signal(
                barrier, inc=1, device_id={axis: me[axis] + (1 if high else -1)}, device_id_type=MESH
            )

    for (axis_a, high_a), (axis_b, high_b) in edge_sides():
        there = exists(axis_a, high_a) & exists(axis_b, high_b)
        expected = expected + there.astype(jnp.int32)

        @pl.when(there)
        def _():
            pl.semaphore_signal(
                barrier, inc=1, device_id=beside((axis_a, high_a), (axis_b, high_b)), device_id_type=MESH
            )

    received = {
        "gx": (xr_fine, xr_coarse, xr_deep),
        "gy": (yr_fine, yr_coarse, yr_deep),
        "agg": (zr_fine, zr_coarse, zr_deep),
    }
    edges = {("gx", "gy"): exy, ("gx", "agg"): exz, ("gy", "agg"): eyz}
    for (axis_a, high_a), (axis_b, high_b) in edge_sides():
        @pl.when(jnp.logical_not(exists(axis_a, high_a) & exists(axis_b, high_b)))
        def _():
            buffer = edges[axis_a, axis_b]
            for phase in range(buffer.shape[0]):
                buffer[phase, 2 * int(high_a) + int(high_b)] = jnp.zeros(buffer.shape[2:], buffer.dtype)

    for buffer in (ys_coarse, ys_deep):
        buffer[...] = jnp.zeros(buffer.shape, buffer.dtype)
    for axis, high in neighbour_sides():
        @pl.when(jnp.logical_not(exists(axis, high)))
        def _():
            for buffer in received[axis]:
                for phase in range(buffer.shape[0]):
                    buffer[phase, int(high)] = jnp.zeros(buffer.shape[2:], buffer.dtype)

    row = lax.broadcasted_iota(jnp.int32, (Y, Z), 0)
    lane = lax.broadcasted_iota(jnp.int32, (Y, Z), 1)
    zero = jnp.zeros((Y, Z), jnp.float32)

    def pack(fields, width, phase, xs, ys, zs):
        packed = zero
        for c in range(C):
            for x in range(width):
                k = c * width + x
                field = fields[c][x]
                ys[phase, 0, k : k + 1] = field[0:1]
                ys[phase, 1, k : k + 1] = field[Y - 1 : Y]
                packed = jnp.where(lane == k, field[:, 0:1], packed)
                packed = jnp.where(lane == half + k, field[:, Z - 1 : Z], packed)
        zs[phase] = packed

    def copies(fine, phase):
        number = phase if fine else SWEEPS + 1 + phase
        xs, xr, ys, yr, zs, zr = (
            (xs_fine, xr_fine, ys_fine, yr_fine, zs_fine, zr_fine)
            if fine
            else (xs_coarse, xr_coarse, ys_coarse, yr_coarse, zs_coarse, zr_coarse)
        )
        made = []
        for slot, (axis, high) in enumerate(neighbour_sides()):
            side = int(high)
            if axis == "gx":
                if fine and phase == 0:
                    src = v_ref.at[:, X - 1 if high else 0]
                else:
                    src = xs.at[phase, side]
                dst = xr.at[phase, 1 - side]
            elif axis == "gy":
                src, dst = ys.at[phase, side], yr.at[phase, 1 - side]
            else:
                src, dst = zs.at[phase], zr.at[phase, 1 - side]
            made.append((
                axis,
                high,
                pltpu.make_async_remote_copy(
                    src_ref=src,
                    dst_ref=dst,
                    send_sem=send_sem.at[number, slot],
                    recv_sem=recv_sem.at[number, slot],
                    device_id={axis: me[axis] + (1 if high else -1)},
                    device_id_type=MESH,
                ),
            ))
        return made

    def start(fine, phase, axes=("gx", "gy", "agg")):
        for axis, high, copy in copies(fine, phase):
            if axis in axes:
                pl.when(exists(axis, high))(copy.start)

    def send(fine, phase, fields, width):
        xs, ys, zs = fine_send if fine else coarse_send
        for c in range(C):
            xs[phase, 0, c] = fields[c][0]
            xs[phase, 1, c] = fields[c][width - 1]
        start(fine, phase, ("gx",))
        pack(fields, width, phase, xs, ys, zs)
        start(fine, phase, ("gy", "agg"))

    def arrive(fine, phase):
        for axis, high, copy in copies(fine, phase):
            pl.when(exists(axis, not high))(copy.wait_recv)

    def sent(fine, phase):
        for axis, high, copy in copies(fine, phase):
            pl.when(exists(axis, high))(copy.wait_send)

    def inner_sum(fields, width, stride):
        sums = []
        for c in range(C):
            line = []
            for x in range(width):
                field = fields[c][x]
                total = jnp.where(row < stride, zero, pltpu.roll(field, stride, 0))
                total = total + jnp.where(row >= Y - stride, zero, pltpu.roll(field, Y - stride, 0))
                total = total + jnp.where(lane < stride, zero, pltpu.roll(field, stride, 1))
                total = total + jnp.where(lane >= Z - stride, zero, pltpu.roll(field, Z - stride, 1))
                if x > 0:
                    total = total + fields[c][x - 1]
                if x < width - 1:
                    total = total + fields[c][x + 1]
                line.append(total)
            sums.append(line)
        return sums

    def outer_sum(sums, width, stride, faces, repeat=1):
        along_x, along_y, along_z = faces
        result = []
        for c in range(C):
            line = []
            for x in range(width):
                k = c * (width // repeat) + x // repeat
                total = sums[c][x]
                total = total + jnp.where(row < stride, along_y[0][k : k + 1], 0.0)
                total = total + jnp.where(row >= Y - stride, along_y[1][k : k + 1], 0.0)
                total = total + jnp.where(lane < stride, along_z[0][:, k : k + 1], 0.0)
                total = total + jnp.where(lane >= Z - stride, along_z[1][:, k : k + 1], 0.0)
                if x == 0:
                    total = total + along_x[0][c]
                if x == width - 1:
                    total = total + along_x[1][c]
                line.append(total)
            result.append(line)
        return result

    def faces_of(xr, yr, zr, phase):
        return (
            [[xr[phase, side, c] for c in range(C)] for side in range(2)],
            [yr[phase, side] for side in range(2)],
            [pltpu.roll(zr[phase, 0], half, 1), zr[phase, 1]],
        )

    group = Z // 4
    far = {0: 2, 1: 0}

    def rows_of(width):
        return -(-C * width // 8) * 8

    def deep_copies(phase):
        made = []
        rows = pl.ds(0, rows_of(X if phase == 0 else Xc))
        for slot, (first, second) in enumerate(edge_sides()):
            number = 2 * int(first[1]) + int(second[1])
            back = 3 - number
            if second[0] == "gy":
                src, dst = ys_deep.at[phase, int(second[1]), 0, rows], exy.at[phase, back, rows]
            else:
                src, dst = zs_deep.at[phase], (exz if first[0] == "gx" else eyz).at[phase, back]
            made.append(((first, second), src, dst, 6 + slot))
        for slot, (axis, high) in enumerate(neighbour_sides()):
            side = int(high)
            if axis == "gx":
                src, dst = xs_deep.at[phase, side], xr_deep.at[phase, 1 - side]
            elif axis == "gy":
                src, dst = ys_deep.at[phase, side, :, rows], yr_deep.at[phase, 1 - side, :, rows]
            else:
                src, dst = zs_deep.at[phase], zr_deep.at[phase, 1 - side]
            made.append((((axis, high),), src, dst, slot))
        return [
            (
                sides,
                pltpu.make_async_remote_copy(
                    src_ref=src,
                    dst_ref=dst,
                    send_sem=deep_send_sem.at[phase, slot],
                    recv_sem=deep_recv_sem.at[phase, slot],
                    device_id=beside(*sides),
                    device_id_type=MESH,
                ),
            )
            for sides, src, dst, slot in made
        ]

    def all_exist(sides, flip):
        there = None
        for axis, high in sides:
            one = exists(axis, high != flip)
            there = one if there is None else there & one
        return there

    def deep_send(phase, fields, width, stride):
        for c in range(C):
            for depth in range(2):
                xs_deep[phase, 0, depth, c] = fields[c][depth]
                xs_deep[phase, 1, depth, c] = fields[c][width - 1 - depth]
        ready = deep_copies(phase)
        packed = zero
        for c in range(C):
            for x in range(width):
                k = c * width + x
                field = fields[c][x]
                for depth in range(2):
                    at = depth * stride
                    ys_deep[phase, 0, depth, k : k + 1] = field[at : at + 1]
                    ys_deep[phase, 1, depth, k : k + 1] = field[Y - 1 - at : Y - at]
                    packed = jnp.where(lane == depth * group + k, field[:, at : at + 1], packed)
                    packed = jnp.where(
                        lane == (2 + depth) * group + k, field[:, Z - 1 - at : Z - at], packed
                    )
        zs_deep[phase] = packed
        for sides, copy in ready:
            pl.when(all_exist(sides, False))(copy.start)

    def deep_arrive(phase):
        for sides, copy in deep_copies(phase):
            pl.when(all_exist(sides, True))(copy.wait_recv)

    def deep_sent(phase):
        for sides, copy in deep_copies(phase):
            pl.when(all_exist(sides, False))(copy.wait_send)

    def lanes_from(packed, number, shift=0):
        turn = (shift - number * group) % Z
        return pltpu.roll(packed, turn, 1) if turn else packed

    def deep_faces(phase):
        return (
            [[xr_deep[phase, side, 0, c] for c in range(C)] for side in range(2)],
            [yr_deep[phase, side, 0, : rows_of(X if phase == 0 else Xc)] for side in range(2)],
            [lanes_from(zr_deep[phase, side], far[side]) for side in range(2)],
        )

    def advance_faces(phase, fields, width, stride, faces, added, weight):
        along_x, along_y, along_z = [], [], []
        rows = rows_of(width)
        k_row = lax.broadcasted_iota(jnp.int32, (rows, Z), 0)
        k_lane = lax.broadcasted_iota(jnp.int32, (rows, Z), 1)
        for side in range(2):
            near = width - 1 if side == 0 else 0
            planes = []
            for c in range(C):
                plane = faces[0][side][c]
                k = c * width + near
                total = xr_deep[phase, side, 1, c] + fields[c][0 if side == 0 else width - 1]
                total = total + jnp.where(
                    row < stride, exy[phase, 2 * side, k : k + 1], pltpu.roll(plane, stride, 0)
                )
                total = total + jnp.where(
                    row >= Y - stride, exy[phase, 2 * side + 1, k : k + 1], pltpu.roll(plane, Y - stride, 0)
                )
                low = exz[phase, 2 * side][:, far[0] * group + k : far[0] * group + k + 1]
                high = exz[phase, 2 * side + 1][:, far[1] * group + k : far[1] * group + k + 1]
                total = total + jnp.where(lane < stride, low, pltpu.roll(plane, stride, 1))
                total = total + jnp.where(lane >= Z - stride, high, pltpu.roll(plane, Z - stride, 1))
                planes.append(keep * plane + added[0][side][c] + weight[0][side][c] * total)
            along_x.append(planes)

            layer = faces[1][side]
            total = yr_deep[phase, side, 1, :rows] + ys_deep[phase, side, 0, :rows]
            spot = k_row % width
            total = total + jnp.where(
                spot == 0, pltpu.roll(exy[phase, side, :rows], rows - (width - 1), 0), pltpu.roll(layer, 1, 0)
            )
            total = total + jnp.where(
                spot == width - 1, pltpu.roll(exy[phase, 2 + side, :rows], width - 1, 0), pltpu.roll(layer, rows - 1, 0)
            )
            at = Y - 1 if side == 0 else 0
            ends = []
            for z_side in range(2):
                line = eyz[phase, 2 * side + z_side, at : at + 1]
                chosen = jnp.where(k_lane == far[z_side] * group + k_row, line, 0.0)
                ends.append(jnp.sum(chosen, axis=1, keepdims=True))
            total = total + jnp.where(k_lane < stride, ends[0], pltpu.roll(layer, stride, 1))
            total = total + jnp.where(k_lane >= Z - stride, ends[1], pltpu.roll(layer, Z - stride, 1))
            along_y.append(keep * layer + added[1][side] + weight[1][side] * total)

            layer = faces[2][side]
            total = lanes_from(zr_deep[phase, side], far[side] + 1)
            total = total + lanes_from(zs_deep[phase], 2 - far[side])
            low = lanes_from(eyz[phase, side], far[side])[Y - 1 : Y]
            high = lanes_from(eyz[phase, 2 + side], far[side])[0:1]
            total = total + jnp.where(row < stride, low, pltpu.roll(layer, stride, 0))
            total = total + jnp.where(row >= Y - stride, high, pltpu.roll(layer, Y - stride, 0))
            spot = lane % width
            total = total + jnp.where(
                spot == 0, lanes_from(exz[phase, side], far[side], 1 - width), pltpu.roll(layer, 1, 1)
            )
            total = total + jnp.where(
                spot == width - 1, lanes_from(exz[phase, 2 + side], far[side], width - 1), pltpu.roll(layer, Z - 1, 1)
            )
            along_z.append(keep * layer + added[2][side] + weight[2][side] * total)
        return along_x, along_y, along_z

    fine_recv = (xr_fine, yr_fine, zr_fine)
    coarse_recv = (xr_coarse, yr_coarse, zr_coarse)
    fine_send = (xs_fine, ys_fine, zs_fine)
    coarse_send = (xs_coarse, ys_coarse, zs_coarse)

    loads[0].wait()
    previous = [[v_ref[c, x] for x in range(X)] for c in range(C)]
    pack(previous, X, 0, *fine_send)
    pl.semaphore_wait(barrier, expected)
    start(True, 0)

    loads[1].wait()
    loads[2].wait()
    for x in range(X):
        w_buf[x] = damping / (6.0 + r_ref[x])
    scaled = [[w_buf[x] * f_ref[c, x] for x in range(X)] for c in range(C)]
    send(True, 1, scaled, X)
    send(True, 2, [[w_buf[x] for x in range(X)]] * C, X)

    kept = X // 2
    parts = Y // 8
    even_row = row % 2 == 0
    even_lane = lane % 2 == 0
    combos_per_tile = Z // chunk
    def c_copy(j, source):
        return pltpu.make_async_remote_copy(
            src_ref=c_send.at[j],
            dst_ref=c_recv.at[source],
            send_sem=c_send_sem.at[j],
            recv_sem=c_recv_sem.at[source],
            device_id={"gx": j},
            device_id_type=MESH,
        )

    def finish_compressed(tiles):
        coefs = blocks * kept
        for tile in tiles:
            gathered = c_recv[:, tile].reshape(coefs * 8, Z)
            done = lax.dot_general(
                m_ref[...], gathered, (((1,), (0,)), ((), ())),
                precision=lax.Precision.HIGHEST, preferred_element_type=jnp.float32,
            )
            for place in range(combos_per_tile):
                c, part = divmod(tile * combos_per_tile + place, parts)
                if c < C:
                    for y in range(8):
                        comp_ref[c, part * 8 + y] = done[
                            y * coefs : (y + 1) * coefs, place * chunk : (place + 1) * chunk
                        ]

    def pooled(planes):
        out = []
        for x in range(0, len(planes), 2):
            total = planes[x] + planes[x + 1]
            total = total + jnp.where(even_row, pltpu.roll(total, Y - 1, 0), pltpu.roll(total, 1, 0))
            total = total + jnp.where(even_lane, pltpu.roll(total, Z - 1, 1), pltpu.roll(total, 1, 1))
            out.append(total * 0.125)
        return out

    coarse_weight = [damping / ((6.0 + 4.0 * mean) * 0.25) for mean in pooled([r_ref[x] for x in range(X)])]
    coarse_step = [0.25 * weight for weight in coarse_weight]

    def fine_sums(current):
        inner = inner_sum(current, X, 1)
        return [[inner[c][x] + f_ref[c, x] for x in range(X)] for c in range(C)]

    def fine_sweep(current, total):
        return [[keep * current[c][x] + w_buf[x] * total[c][x] for x in range(X)] for c in range(C)]

    sums = fine_sums(previous)
    arrive(True, 0)
    field = fine_sweep(previous, outer_sum(sums, X, 1, faces_of(*fine_recv, 0)))
    deep_send(0, field, X, 1)
    send(False, 0, [coarse_step] * C, Xc)

    levels = local_levels(X)
    coefficients = []
    for c in range(C):
        approx, details = previous[c], []
        for level in range(levels):
            low, high = approx[0::2], approx[1::2]
            approx = [(a + b) * root_half for a, b in zip(low, high)]
            if level > 0:
                details = [(a - b) * root_half for a, b in zip(low, high)] + details
        line = []
        for values in approx + details:
            swapped = jnp.where(even_lane, pltpu.roll(values, Z - 1, 1), pltpu.roll(values, 1, 1))
            line.append((jnp.where(even_lane, values, -values) + swapped) * root_half)
        coefficients.append(line)
    row8 = lax.broadcasted_iota(jnp.int32, (8, Z), 1)
    for j in range(blocks):
        for k in range(kept):
            tiles = {}
            for c in range(C):
                for part in range(parts):
                    tile, place = divmod(c * parts + part, combos_per_tile)
                    values = coefficients[c][k][part * 8 : part * 8 + 8]
                    shift = (place * chunk - j * chunk) % Z
                    moved = pltpu.roll(values, shift, 1) if shift else values
                    if tile in tiles:
                        moved = jnp.where((row8 >= place * chunk) & (row8 < (place + 1) * chunk), moved, tiles[tile])
                    tiles[tile] = moved
            for tile, value in tiles.items():
                c_send[j, tile, k] = value

    for j in range(blocks):
        pl.when(me["gx"] != j)(c_copy(j, me["gx"]).start)

        @pl.when(me["gx"] == j)
        def _():
            c_recv[j] = c_send[j]

    sums = fine_sums(field)
    arrive(True, 1)
    arrive(True, 2)
    deep_arrive(0)
    faces = deep_faces(0)
    later_faces = advance_faces(
        0, field, X, 1, faces, faces_of(*fine_recv, 1), faces_of(*fine_recv, 2)
    )
    field = fine_sweep(field, outer_sum(sums, X, 1, faces))
    sums = outer_sum(fine_sums(field), X, 1, later_faces)
    coarse_rhs = [
        pooled([sums[c][x] - (6.0 + r_ref[x]) * field[c][x] for x in range(X)]) for c in range(C)
    ]
    correction = [[coarse_weight[x] * coarse_rhs[c][x] for x in range(Xc)] for c in range(C)]
    deep_send(1, correction, Xc, 2)
    for j in range(blocks):
        pl.when(me["gx"] != j)(c_copy(j, j).wait_recv)
    loads[3].wait()
    tiles_here = c_send.shape[1]
    first_tiles = (tiles_here + 1) // 2
    finish_compressed(range(first_tiles))

    def coarse_sweep(current, faces):
        total = outer_sum(inner_sum(current, Xc, 2), Xc, 2, faces)
        return [
            [keep * current[c][x] + first[c][x] + coarse_step[x] * total[c][x] for x in range(Xc)]
            for c in range(C)
        ]

    first = correction
    arrive(False, 0)
    step_faces = faces_of(*coarse_recv, 0)
    deep_arrive(1)
    first_faces = deep_faces(1)
    later_faces = advance_faces(1, correction, Xc, 2, first_faces, first_faces, step_faces)
    correction = coarse_sweep(coarse_sweep(correction, first_faces), later_faces)
    deep_send(2, correction, Xc, 2)
    finish_compressed(range(first_tiles, tiles_here))
    deep_arrive(2)
    faces = deep_faces(2)
    later_faces = advance_faces(2, correction, Xc, 2, faces, first_faces, step_faces)
    correction = coarse_sweep(correction, faces)
    spread = [[correction[c][x // 2] for x in range(X)] for c in range(C)]
    added = inner_sum(spread, X, 1)
    sums = [[sums[c][x] + added[c][x] for x in range(X)] for c in range(C)]
    sums = outer_sum(sums, X, 1, later_faces, repeat=2)
    for c in range(C):
        for x in range(X):
            vel_ref[c, x] = keep * (field[c][x] + spread[c][x]) + w_buf[x] * sums[c][x]

    for phase in range(SWEEPS + 1):
        sent(True, phase)
    sent(False, 0)
    for phase in range(1 + COARSE_SWEEPS // 2):
        deep_sent(phase)
    for j in range(blocks):
        pl.when(me["gx"] != j)(c_copy(j, me["gx"]).wait_send)


def on_device(counts, velocity_prev, forcing, reaction):
    C, X, Y, Z = velocity_prev.shape
    blocks = counts["gx"]
    kept = X // 2
    chunk = Z // blocks
    tiles = -(-(C * (Y // 8)) // (Z // chunk))
    matrix = jnp.asarray(finish_matrix(X, blocks, 8))
    vmem = pl.BlockSpec(memory_space=pltpu.VMEM)

    def buffers(phases, width):
        return [
            pltpu.VMEM((phases, 2, C, Y, Z), jnp.float32),
            pltpu.VMEM((phases, 2, C, Y, Z), jnp.float32),
            pltpu.VMEM((phases, 2, -(-C * width // 8) * 8, Z), jnp.float32),
            pltpu.VMEM((phases, 2, -(-C * width // 8) * 8, Z), jnp.float32),
            pltpu.VMEM((phases, Y, Z), jnp.float32),
            pltpu.VMEM((phases, 2, Y, Z), jnp.float32),
        ]

    def deep_buffers(phases, width):
        rows = -(-C * width // 8) * 8
        return [
            pltpu.VMEM((phases, 2, 2, C, Y, Z), jnp.float32),
            pltpu.VMEM((phases, 2, 2, C, Y, Z), jnp.float32),
            pltpu.VMEM((phases, 2, 2, rows, Z), jnp.float32),
            pltpu.VMEM((phases, 2, 2, rows, Z), jnp.float32),
            pltpu.VMEM((phases, Y, Z), jnp.float32),
            pltpu.VMEM((phases, 2, Y, Z), jnp.float32),
            pltpu.VMEM((phases, 4, rows, Z), jnp.float32),
            pltpu.VMEM((phases, 4, Y, Z), jnp.float32),
            pltpu.VMEM((phases, 4, Y, Z), jnp.float32),
        ]

    phases = SWEEPS + 2
    velocity, compressed = pl.pallas_call(
        functools.partial(kernel, counts),
        out_shape=(
            jax.ShapeDtypeStruct((C, X, Y, Z), jnp.float32),
            jax.ShapeDtypeStruct((C, Y, kept * blocks, chunk), jnp.float32),
        ),
        in_specs=[pl.BlockSpec(memory_space=pltpu.HBM)] * 4,
        out_specs=(vmem, vmem),
        scratch_shapes=[
            pltpu.VMEM((C, X, Y, Z), jnp.float32),
            pltpu.VMEM((C, X, Y, Z), jnp.float32),
            pltpu.VMEM((X, Y, Z), jnp.float32),
            pltpu.VMEM(matrix.shape, jnp.float32),
        ] + buffers(SWEEPS + 1, X) + buffers(1, X // 2) + deep_buffers(1 + COARSE_SWEEPS // 2, X) + [
            pltpu.VMEM((blocks, tiles, kept, 8, Z), jnp.float32),
            pltpu.VMEM((blocks, tiles, kept, 8, Z), jnp.float32),
            pltpu.VMEM((X, Y, Z), jnp.float32),
            pltpu.SemaphoreType.DMA((phases, 6)),
            pltpu.SemaphoreType.DMA((phases, 6)),
            pltpu.SemaphoreType.DMA((1 + COARSE_SWEEPS // 2, 18)),
            pltpu.SemaphoreType.DMA((1 + COARSE_SWEEPS // 2, 18)),
            pltpu.SemaphoreType.DMA((blocks,)),
            pltpu.SemaphoreType.DMA((blocks,)),
            pltpu.SemaphoreType.DMA((4,)),
        ],
        compiler_params=pltpu.CompilerParams(collective_id=0, has_side_effects=True, vmem_limit_bytes=40000000),
    )(*(pltpu.with_memory_space_constraint(a, pltpu.HBM) for a in (velocity_prev, forcing, reaction, matrix)))
    return velocity, jnp.swapaxes(compressed, 2, 3)


def solution(mesh):
    counts = {axis: mesh.shape[axis] for axis in ("agg", "gx", "gy")}
    placed = (P(None, "gx", "gy", "agg"), P(None, "gx", "gy", "agg"), P("gx", "gy", "agg"))
    return jax.shard_map(
        functools.partial(on_device, counts),
        mesh=mesh,
        in_specs=placed,
        out_specs=(P(None, "gx", "gy", "agg"), P(None, "gy", ("agg", "gx"), None)),
        check_vma=False,
    )
```

profile of v0, /device:TPU:0, one launch (start us, length us, event | category | flops | bytes accessed | tf_op | source)
XLA Modules:
  0.0 24.1 jit_solution(7448711787001251484)
XLA Ops:
  0.6 22.1 %shard_map.59 = (f32[3,8,16,128]{3,2,1,0:T(8,128)S(1)}, f32[3,16,16,32]{3,2,1,0:T(8,128)S(1)}) custom-call(f32[3,8,16,128]{3,2,1,0:T(8,128)} %v_hbm.1, f32[3,8,16,128]{3,2,1,0:T(8,128)} %f_hbm.1, f32[8,16,128]{2,1,0:T(8,128)} %r_hbm.1, f32[128,128]{1,0:T(8,128)} %constant.2.clone.m_hbm), custom_call_target="tpu_custom_call" | custom-call | tf_op jit(solution)/shard_map/pallas_call | solution.py:607
  22.7 0.7 %copy.8 = f32[3,8,16,128]{3,2,1,0:T(8,128)} copy(f32[3,8,16,128]{3,2,1,0:T(8,128)S(1)} %get-tuple-element.8) | data formatting | bytes 393216
  23.4 0.7 %copy.9 = f32[3,16,32,16]{2,3,1,0:T(8,128)} copy(f32[3,16,32,16]{2,3,1,0:T(8,128)S(1)} %bitcast.1) | data formatting | bytes 196608
where the time goes:
time: 24.3 us; the launch traced here: 24.1 us
  Pallas kernels  22.1 us (91%)
  local copies, waits for them, and re-layouts  1.42 us (6%)
  between operations  0.64 us (3%)
    pallas_call x1, Pallas kernels, on_device(): pl.pallas_call(functools.partial(kernel, counts), out_shape=(jax.ShapeDty...  22.1 us
    unnamed x2, local copies, waits for them, and re-layouts  1.42 us

commit v1 on v0

--- a/solution.py
+++ b/solution.py
@@ -54,12 +54,22 @@
     return [((a, p), (b, q)) for a, b in pairs for p in (False, True) for q in (False, True)]
 
 
+def around():
+    axes = ("gx", "gy", "agg")
+    found = []
+    for number in range(1, 27):
+        turn = [(number // 3**i) % 3 for i in range(3)]
+        found.append(tuple((axis, way == 1) for axis, way in zip(axes, turn) if way))
+    return sorted(found, key=lambda sides: (-len(sides), sides))
+
+
 def kernel(
     sizes, v_hbm, f_hbm, r_hbm, m_hbm, vel_ref, comp_ref, v_ref, f_ref, r_ref, m_ref,
     xs_fine, xr_fine, ys_fine, yr_fine, zs_fine, zr_fine,
-    xs_coarse, xr_coarse, ys_coarse, yr_coarse, zs_coarse, zr_coarse,
+    q_ext, h_ext, zs_coarse,
     xs_deep, xr_deep, ys_deep, yr_deep, zs_deep, zr_deep, exy, exz, eyz,
-c_send, c_recv, w_buf, send_sem, recv_sem, deep_send_sem, deep_recv_sem, c_send_sem, c_recv_sem, in_sem,
+c_send, c_recv, w_buf, send_sem, recv_sem, deep_send_sem, deep_recv_sem, q_send_sem, q_recv_sem,
+    c_send_sem, c_recv_sem, in_sem,
 ):
     counts = sizes
     C, X, Y, Z = v_ref.shape
@@ -89,30 +99,60 @@
         pl.semaphore_signal(
             barrier, inc=1, device_id={"gx": lax.rem(me["gx"] + step, blocks)}, device_id_type=MESH
         )
-    for axis, high in neighbour_sides()[2:]:
-        there = exists(axis, high)
-        expected = expected + there.astype(jnp.int32)
-
-        @pl.when(there)
+    def all_exist(sides, flip):
+        there = None
+        for axis, high in sides:
+            one = exists(axis, high != flip)
+            there = one if there is None else there & one
+        return there
+
+    for sides in around():
+        if len(sides) > 1 or sides[0][0] != "gx":
+            there = all_exist(sides, False)
+            expected = expected + there.astype(jnp.int32)
+
+            @pl.when(there)
+            def _():
+                pl.semaphore_signal(barrier, inc=1, device_id=beside(*sides), device_id_type=MESH)
+
+    def coarse_message(sides):
+        at = {axis: 1 if high else -1 for axis, high in sides}
+        block = 1 - at.get("gx", 0)
+        here, there = {
+            0: (slice(0, Y), slice(0, Y)),
+            1: (slice(Y - 8, Y), slice(Y + 8, Y + 16)),
+            -1: (slice(0, 8), slice(Y, Y + 8)),
+        }[at.get("gy", 0)]
+        if "agg" in at:
+            return zs_coarse.at[here], h_ext.at[0 if at["agg"] > 0 else 1, block, there]
+        return q_ext.at[1, :, here], q_ext.at[block, :, there]
+
+    def coarse_copies():
+        return [
+            (
+                sides,
+                pltpu.make_async_remote_copy(
+                    src_ref=coarse_message(sides)[0],
+                    dst_ref=coarse_message(sides)[1],
+                    send_sem=q_send_sem.at[slot],
+                    recv_sem=q_recv_sem.at[slot],
+                    device_id=beside(*sides),
+                    device_id_type=MESH,
+                ),
+            )
+            for slot, sides in enumerate(around())
+        ]
+
+    for sides in around():
+        @pl.when(jnp.logical_not(all_exist(sides, True)))
         def _():
-            pl.semaphore_signal(
-                barrier, inc=1, device_id={axis: me[axis] + (1 if high else -1)}, device_id_type=MESH
-            )
-
-    for (axis_a, high_a), (axis_b, high_b) in edge_sides():
-        there = exists(axis_a, high_a) & exists(axis_b, high_b)
-        expected = expected + there.astype(jnp.int32)
-
-        @pl.when(there)
-        def _():
-            pl.semaphore_signal(
-                barrier, inc=1, device_id=beside((axis_a, high_a), (axis_b, high_b)), device_id_type=MESH
-            )
+            target = coarse_message(sides)[1]
+            target[...] = jnp.zeros(target.shape, jnp.float32)
 
     received = {
-        "gx": (xr_fine, xr_coarse, xr_deep),
-        "gy": (yr_fine, yr_coarse, yr_deep),
-        "agg": (zr_fine, zr_coarse, zr_deep),
+        "gx": (xr_fine, xr_deep),
+        "gy": (yr_fine, yr_deep),
+        "agg": (zr_fine, zr_deep),
     }
     edges = {("gx", "gy"): exy, ("gx", "agg"): exz, ("gy", "agg"): eyz}
     for (axis_a, high_a), (axis_b, high_b) in edge_sides():
@@ -122,8 +162,7 @@
             for phase in range(buffer.shape[0]):
                 buffer[phase, 2 * int(high_a) + int(high_b)] = jnp.zeros(buffer.shape[2:], buffer.dtype)
 
-    for buffer in (ys_coarse, ys_deep):
-        buffer[...] = jnp.zeros(buffer.shape, buffer.dtype)
+    ys_deep[...] = jnp.zeros(ys_deep.shape, ys_deep.dtype)
     for axis, high in neighbour_sides():
         @pl.when(jnp.logical_not(exists(axis, high)))
         def _():
@@ -148,12 +187,8 @@
         zs[phase] = packed
 
     def copies(fine, phase):
-        number = phase if fine else SWEEPS + 1 + phase
-        xs, xr, ys, yr, zs, zr = (
-            (xs_fine, xr_fine, ys_fine, yr_fine, zs_fine, zr_fine)
-            if fine
-            else (xs_coarse, xr_coarse, ys_coarse, yr_coarse, zs_coarse, zr_coarse)
-        )
+        number = phase
+        xs, xr, ys, yr, zs, zr = xs_fine, xr_fine, ys_fine, yr_fine, zs_fine, zr_fine
         made = []
         for slot, (axis, high) in enumerate(neighbour_sides()):
             side = int(high)
@@ -187,7 +222,7 @@
                 pl.when(exists(axis, high))(copy.start)
 
     def send(fine, phase, fields, width):
-        xs, ys, zs = fine_send if fine else coarse_send
+        xs, ys, zs = fine_send
         for c in range(C):
             xs[phase, 0, c] = fields[c][0]
             xs[phase, 1, c] = fields[c][width - 1]
@@ -289,13 +324,6 @@
             for sides, src, dst, slot in made
         ]
 
-    def all_exist(sides, flip):
-        there = None
-        for axis, high in sides:
-            one = exists(axis, high != flip)
-            there = one if there is None else there & one
-        return there
-
     def deep_send(phase, fields, width, stride):
         for c in range(C):
             for depth in range(2):
@@ -400,9 +428,7 @@
         return along_x, along_y, along_z
 
     fine_recv = (xr_fine, yr_fine, zr_fine)
-    coarse_recv = (xr_coarse, yr_coarse, zr_coarse)
     fine_send = (xs_fine, ys_fine, zs_fine)
-    coarse_send = (xs_coarse, ys_coarse, zs_coarse)
 
     loads[0].wait()
     previous = [[v_ref[c, x] for x in range(X)] for c in range(C)]
@@ -449,17 +475,45 @@
                             y * coefs : (y + 1) * coefs, place * chunk : (place + 1) * chunk
                         ]
 
+    tiles_y = Y // 8
+    lane8 = lax.broadcasted_iota(jnp.int32, (8, Z), 1)
+    row_in = lax.broadcasted_iota(jnp.int32, (8, Z), 0)
+    even_l = lane8 % 2 == 0
+    even_r = row_in % 2 == 0
+    slot_at = lane8 % 16
+    lane_roll = lambda t, shift: pltpu.roll(t, shift % Z, 1) if shift % Z else t
+    row_roll = lambda t, shift: pltpu.roll(t, shift % 8, 0)
+    lane_swap = lambda t: jnp.where(even_l, lane_roll(t, -1), lane_roll(t, 1))
+    row_swap = lambda t: jnp.where(even_r, row_roll(t, -1), row_roll(t, 1))
+    corner_of = ((0, 0), (0, 1), (1, 1), (1, 0))
+
     def pooled(planes):
+        pairs = [planes[x] + planes[x + 1] for x in range(0, X, 2)]
         out = []
-        for x in range(0, len(planes), 2):
-            total = planes[x] + planes[x + 1]
-            total = total + jnp.where(even_row, pltpu.roll(total, Y - 1, 0), pltpu.roll(total, 1, 0))
-            total = total + jnp.where(even_lane, pltpu.roll(total, Z - 1, 1), pltpu.roll(total, 1, 1))
-            out.append(total * 0.125)
+        for t in range(tiles_y):
+            t0, t1, t2, t3 = (pair[t * 8 : t * 8 + 8] for pair in pairs)
+            left = jnp.where(even_r, t0, t3) + row_swap(jnp.where(even_r, t3, t0))
+            right = jnp.where(even_r, t1, t2) + row_swap(jnp.where(even_r, t2, t1))
+            out.append(jnp.where(even_l, left, right) + lane_swap(jnp.where(even_l, right, left)))
         return out
 
-    coarse_weight = [damping / ((6.0 + 4.0 * mean) * 0.25) for mean in pooled([r_ref[x] for x in range(X)])]
+    def edge_lanes(fields, t):
+        packed = jnp.zeros((8, Z), jnp.float32)
+        for start, field in fields:
+            for depth in range(1, 5):
+                high = (lane8 >= start + 8 - 2 * depth) & (lane8 < start + 10 - 2 * depth)
+                packed = jnp.where(high, lane_roll(field[t], start + 10 - 4 * depth), packed)
+                low = (lane8 >= start + 6 + 2 * depth) & (lane8 < start + 8 + 2 * depth)
+                packed = jnp.where(low, lane_roll(field[t], start + 6 + 4 * depth), packed)
+        return packed
+
+    coarse_weight = [
+        damping / ((6.0 + 0.5 * total) * 0.25) for total in pooled([r_ref[x] for x in range(X)])
+    ]
     coarse_step = [0.25 * weight for weight in coarse_weight]
+    step_edges = [edge_lanes([(64 + 16 * c, coarse_step) for c in range(C)], t) for t in range(tiles_y)]
+    for t in range(tiles_y):
+        q_ext[1, C, t * 8 : t * 8 + 8] = coarse_step[t]
 
     def fine_sums(current):
         inner = inner_sum(current, X, 1)
@@ -472,7 +526,6 @@
     arrive(True, 0)
     field = fine_sweep(previous, outer_sum(sums, X, 1, faces_of(*fine_recv, 0)))
     deep_send(0, field, X, 1)
-    send(False, 0, [coarse_step] * C, Xc)
 
     levels = local_levels(X)
     coefficients = []
@@ -521,51 +574,126 @@
     )
     field = fine_sweep(field, outer_sum(sums, X, 1, faces))
     sums = outer_sum(fine_sums(field), X, 1, later_faces)
-    coarse_rhs = [
-        pooled([sums[c][x] - (6.0 + r_ref[x]) * field[c][x] for x in range(X)]) for c in range(C)
-    ]
-    correction = [[coarse_weight[x] * coarse_rhs[c][x] for x in range(Xc)] for c in range(C)]
-    deep_send(1, correction, Xc, 2)
+    correction = []
+    for c in range(C):
+        rhs = pooled([sums[c][x] - (6.0 + r_ref[x]) * field[c][x] for x in range(X)])
+        correction.append([weight * (0.125 * total) for weight, total in zip(coarse_weight, rhs)])
+    for c in range(C):
+        for t in range(tiles_y):
+            q_ext[1, c, t * 8 : t * 8 + 8] = correction[c][t]
+    for t in range(tiles_y):
+        edges_t = edge_lanes([(16 * c, correction[c]) for c in range(C)], t)
+        zs_coarse[t * 8 : t * 8 + 8] = jnp.where(lane8 < 64, edges_t, step_edges[t])
+    for sides, copy in coarse_copies():
+        pl.when(all_exist(sides, False))(copy.start)
+
     for j in range(blocks):
         pl.when(me["gx"] != j)(c_copy(j, j).wait_recv)
     loads[3].wait()
-    tiles_here = c_send.shape[1]
-    first_tiles = (tiles_here + 1) // 2
-    finish_compressed(range(first_tiles))
-
-    def coarse_sweep(current, faces):
-        total = outer_sum(inner_sum(current, Xc, 2), Xc, 2, faces)
-        return [
-            [keep * current[c][x] + first[c][x] + coarse_step[x] * total[c][x] for x in range(Xc)]
-            for c in range(C)
-        ]
-
-    first = correction
-    arrive(False, 0)
-    step_faces = faces_of(*coarse_recv, 0)
-    deep_arrive(1)
-    first_faces = deep_faces(1)
-    later_faces = advance_faces(1, correction, Xc, 2, first_faces, first_faces, step_faces)
-    correction = coarse_sweep(coarse_sweep(correction, first_faces), later_faces)
-    deep_send(2, correction, Xc, 2)
-    finish_compressed(range(first_tiles, tiles_here))
-    deep_arrive(2)
-    faces = deep_faces(2)
-    later_faces = advance_faces(2, correction, Xc, 2, faces, first_faces, step_faces)
-    correction = coarse_sweep(correction, faces)
-    spread = [[correction[c][x // 2] for x in range(X)] for c in range(C)]
-    added = inner_sum(spread, X, 1)
-    sums = [[sums[c][x] + added[c][x] for x in range(X)] for c in range(C)]
-    sums = outer_sum(sums, X, 1, later_faces, repeat=2)
+    finish_compressed(range(c_send.shape[1]))
+
+    for sides, copy in coarse_copies():
+        pl.when(all_exist(sides, True))(copy.wait_recv)
+
+    near, ring = range(tiles_y), range(tiles_y + 2)
+    after = lambda t: (t + 1) % len(ring)
+    before = lambda t: (t - 1) % len(ring)
+    tile_of = lambda t: slice(t * 8, t * 8 + 8)
+    main = {(b, c, t): q_ext[b, c, tile_of(t)] for b in range(3) for c in range(C) for t in ring}
+    step_main = {(b, t): q_ext[b, C, tile_of(t)] for b in range(3) for t in ring}
+    edge = {
+        (b, t): jnp.where(slot_at < 8, h_ext[1, b, tile_of(t)], h_ext[0, b, tile_of(t)])
+        for b in range(3) for t in ring
+    }
+    step_edge = {key: lane_roll(value, -64) for key, value in edge.items()}
+    first_main, first_edge = dict(main), dict(edge)
+
+    def above(get, t):
+        return jnp.where(row_in < 6, row_roll(get(t), -2), row_roll(get(after(t)), -2))
+
+    def below(get, t):
+        return jnp.where(row_in >= 2, row_roll(get(t), 2), row_roll(get(before(t)), 2))
+
+    def along(get, b, t):
+        low, high = get(max(b - 1, 0), t), get(min(b + 1, 2), t)
+        across = jnp.where(even_l, jnp.where(even_r, high, low), get(b, t))
+        return lane_swap(get(b, t)) + row_swap(across)
+
+    def inject(edge, b, c, t):
+        return lane_roll(edge[b, t], -(16 * c + 8))
+
+    def left_of(main, edge, b, c, t):
+        return jnp.where(lane8 < 2, inject(edge, b, c, t), lane_roll(main[b, c, t], 2))
+
+    def right_of(main, edge, b, c, t):
+        return jnp.where(lane8 >= Z - 2, inject(edge, b, c, t), lane_roll(main[b, c, t], -2))
+
+    def coarse_sweep(main, edge, main_at, edge_at):
+        new_main, new_edge = dict(main), dict(edge)
+        for b, t in main_at:
+            for c in range(C):
+                get = lambda b, t, c=c: main[b, c, t]
+                row_get = lambda t, b=b, c=c: main[b, c, t]
+                total = along(get, b, t) + (above(row_get, t) + below(row_get, t))
+                total = total + (left_of(main, edge, b, c, t) + right_of(main, edge, b, c, t))
+                new_main[b, c, t] = keep * main[b, c, t] + first_main[b, c, t] + step_main[b, t] * total
+        for b, t in edge_at:
+            get = lambda b, t: edge[b, t]
+            row_get = lambda t, b=b: edge[b, t]
+            own = lane_roll(main[b, 0, t], 8)
+            for c in range(1, C):
+                own = jnp.where(lane8 < 16 * c, own, lane_roll(main[b, c, t], 16 * c + 8))
+            total = along(get, b, t) + (above(row_get, t) + below(row_get, t))
+            total = total + jnp.where((slot_at == 8) | (slot_at == 9), own, lane_roll(edge[b, t], 2))
+            total = total + jnp.where((slot_at == 6) | (slot_at == 7), own, lane_roll(edge[b, t], -2))
+            new_edge[b, t] = keep * edge[b, t] + first_edge[b, t] + step_edge[b, t] * total
+        return new_main, new_edge
+
+    everywhere = [(b, t) for b in range(3) for t in ring]
+    centre = [(1, t) for t in ring]
+    sides_near = [(b, t) for b in (0, 2) for t in near]
+    main, edge = coarse_sweep(main, edge, everywhere, everywhere)
+    main, edge = coarse_sweep(main, edge, everywhere, centre + sides_near)
+    main, edge = coarse_sweep(main, edge, centre + sides_near, [(1, t) for t in near])
+
+    def spread_rows(even, odd, pa):
+        if pa == 0:
+            return jnp.where(even_r, even, row_roll(odd, 1))
+        return jnp.where(even_r, row_roll(even, -1), odd)
+
+    def spread_lanes(even, odd, pb):
+        if pb == 0:
+            return jnp.where(even_l, even, lane_roll(odd, 1))
+        return jnp.where(even_l, lane_roll(even, -1), odd)
+
     for c in range(C):
-        for x in range(X):
-            vel_ref[c, x] = keep * (field[c][x] + spread[c][x]) + w_buf[x] * sums[c][x]
+        for t in near:
+            at = tile_of(t)
+            row_get = lambda t, c=c: main[1, c, t]
+            own = main[1, c, t]
+            rows_near = (below(row_get, t), above(row_get, t))
+            lanes_near = (left_of(main, edge, 1, c, t), right_of(main, edge, 1, c, t))
+            alone = [spread_lanes(own, own, pb) for pb in range(2)]
+            spread = [spread_rows(alone[pb], alone[pb], pa) for pa, pb in corner_of]
+            low, high = (spread_lanes(main[b, c, t], main[b, c, t], 0) for b in (0, 2))
+            spread = [spread_rows(low, low, 1)] + spread + [spread_rows(high, high, 0)]
+            based = [3.0 * own + rows_near[a] for a in range(2)]
+            wide = [
+                [spread_lanes(based[a] + lanes_near[0], based[a] + lanes_near[1], pb) for pb in range(2)]
+                for a in range(2)
+            ]
+            for x in range(X):
+                p = x // 2
+                pa, pb = corner_of[p]
+                added = spread_rows(wide[0][pb], wide[1][pb], pa) + spread[p + 2 * (x % 2)]
+                total = sums[c][x][at] + added
+                vel_ref[c, x, at] = keep * (field[c][x][at] + spread[p + 1]) + w_buf[x, at] * total
 
     for phase in range(SWEEPS + 1):
         sent(True, phase)
-    sent(False, 0)
-    for phase in range(1 + COARSE_SWEEPS // 2):
-        deep_sent(phase)
+    deep_sent(0)
+    for sides, copy in coarse_copies():
+        pl.when(all_exist(sides, False))(copy.wait_send)
     for j in range(blocks):
         pl.when(me["gx"] != j)(c_copy(j, me["gx"]).wait_send)
 
@@ -603,7 +731,7 @@
             pltpu.VMEM((phases, 4, Y, Z), jnp.float32),
         ]
 
-    phases = SWEEPS + 2
+    phases = SWEEPS + 1
     velocity, compressed = pl.pallas_call(
         functools.partial(kernel, counts),
         out_shape=(
@@ -617,14 +745,20 @@
             pltpu.VMEM((C, X, Y, Z), jnp.float32),
             pltpu.VMEM((X, Y, Z), jnp.float32),
             pltpu.VMEM(matrix.shape, jnp.float32),
-        ] + buffers(SWEEPS + 1, X) + buffers(1, X // 2) + deep_buffers(1 + COARSE_SWEEPS // 2, X) + [
+        ] + buffers(SWEEPS + 1, X) + [
+            pltpu.VMEM((3, C + 1, Y + 16, Z), jnp.float32),
+            pltpu.VMEM((2, 3, Y + 16, Z), jnp.float32),
+            pltpu.VMEM((Y, Z), jnp.float32),
+        ] + deep_buffers(1, X) + [
             pltpu.VMEM((blocks, tiles, kept, 8, Z), jnp.float32),
             pltpu.VMEM((blocks, tiles, kept, 8, Z), jnp.float32),
             pltpu.VMEM((X, Y, Z), jnp.float32),
             pltpu.SemaphoreType.DMA((phases, 6)),
             pltpu.SemaphoreType.DMA((phases, 6)),
-            pltpu.SemaphoreType.DMA((1 + COARSE_SWEEPS // 2, 18)),
-            pltpu.SemaphoreType.DMA((1 + COARSE_SWEEPS // 2, 18)),
+            pltpu.SemaphoreType.DMA((1, 18)),
+            pltpu.SemaphoreType.DMA((1, 18)),
+            pltpu.SemaphoreType.DMA((26,)),
+            pltpu.SemaphoreType.DMA((26,)),
             pltpu.SemaphoreType.DMA((blocks,)),
             pltpu.SemaphoreType.DMA((blocks,)),
             pltpu.SemaphoreType.DMA((4,)),

time: 24.3 us -> 20.7 us (0.85)
  Pallas kernels: 22.1 us -> 18.5 us
    pallas_call x1, Pallas kernels: 22.1 us -> 18.5 us  [on_device(): pl.pallas_call(functools.partial(kernel, counts), out_shape=(jax.ShapeDty...]
where the time goes in v1:
time: 20.7 us; the launch traced here: 20.5 us
  Pallas kernels  18.5 us (89%)
  local copies, waits for them, and re-layouts  1.42 us (7%)
  between operations  0.64 us (3%)
    pallas_call x1, Pallas kernels, on_device(): pl.pallas_call(functools.partial(kernel, counts), out_shape=(jax.ShapeDty...  18.5 us
    unnamed x2, local copies, waits for them, and re-layouts  1.42 us

profile of v1, /device:TPU:0, one launch (start us, length us, event | category | flops | bytes accessed | tf_op | source)
XLA Modules:
  0.0 20.5 jit_solution(1625349120836260556)
XLA Ops:
  0.6 18.5 %shard_map.59 = (f32[3,8,16,128]{3,2,1,0:T(8,128)S(1)}, f32[3,16,16,32]{3,2,1,0:T(8,128)S(1)}) custom-call(f32[3,8,16,128]{3,2,1,0:T(8,128)} %v_hbm.1, f32[3,8,16,128]{3,2,1,0:T(8,128)} %f_hbm.1, f32[8,16,128]{2,1,0:T(8,128)} %r_hbm.1, f32[128,128]{1,0:T(8,128)} %constant.2.clone.m_hbm), custom_call_target="tpu_custom_call" | custom-call | tf_op jit(solution)/shard_map/pallas_call | solution.py:735
  19.1 0.7 %copy.8 = f32[3,8,16,128]{3,2,1,0:T(8,128)} copy(f32[3,8,16,128]{3,2,1,0:T(8,128)S(1)} %get-tuple-element.8) | data formatting | bytes 393216
  19.8 0.7 %copy.9 = f32[3,16,32,16]{2,3,1,0:T(8,128)} copy(f32[3,16,32,16]{2,3,1,0:T(8,128)S(1)} %bitcast.1) | data formatting | bytes 196608

commit v2 on v1

v2 whole, which is shorter than its diff:
```python
import functools

import jax
import jax.numpy as jnp
import numpy as np
from jax import lax
from jax.experimental import pallas as pl
from jax.experimental.pallas import tpu as pltpu
from jax.sharding import PartitionSpec as P

SWEEPS = 2
COARSE_SWEEPS = 4
LX = 5
MESH = pl.DeviceIdType.MESH

damping = 0.8
keep = 1.0 - damping
root_half = 0.7071067811865476


def local_levels(cells_x):
    return min(LX, cells_x.bit_length() - 1)


def finish_matrix(cells_x, blocks, rows):
    levels = local_levels(cells_x)
    kept = cells_x // 2
    eye = np.eye(blocks * kept).reshape(blocks, kept, blocks * kept)
    width = cells_x >> levels
    approx = eye[:, :width].reshape(blocks * width, -1)
    details, at = [], width
    for level in range(levels, 1, -1):
        width = cells_x >> level
        details.append(eye[:, at : at + width].reshape(blocks * width, -1))
        at += width
    for level in range(levels, LX):
        low, high = approx[0::2], approx[1::2]
        approx, detail = (low + high) * root_half, (low - high) * root_half
        details.insert(0, detail)
    along_x = np.concatenate([approx] + details, axis=0)
    along_y = np.zeros((rows, rows))
    for row in range(0, rows, 2):
        along_y[row, row : row + 2] = root_half
        along_y[row + 1, row : row + 2] = root_half, -root_half
    return np.einsum("qk,yr->yqkr", along_x, along_y).reshape(-1, blocks * kept * rows).astype(np.float32)


def around():
    axes = ("gx", "gy", "agg")
    found = []
    for number in range(1, 27):
        turn = [(number // 3**i) % 3 for i in range(3)]
        found.append(tuple((axis, way == 1) for axis, way in zip(axes, turn) if way))
    return sorted(found, key=lambda sides: (-len(sides), sides))


far = 1e30


def kernel(
    sizes, v_hbm, f_hbm, r_hbm, m_hbm, vel_ref, comp_ref, v_ext, f_ext, r_ext, m_ref, w_ext, u1_ext, u2_ext,
    y_send, y_recv, xy_send, xy_recv, z_send, z_recv, yz_send, yz_recv, xz_send, xz_recv, corner_recv,
    q_ext, h_ext, zs_coarse, c_send, c_recv,
    a_send_sem, a_recv_sem, q_send_sem, q_recv_sem, c_send_sem, c_recv_sem, in_sem,
):
    counts = sizes
    C, X, Y, Z = vel_ref.shape
    me = {axis: lax.axis_index(axis) for axis in counts}
    blocks = counts["gx"]
    chunk = Z // blocks
    rows_ext = Y + 8
    f32 = jnp.float32

    loads = [
        pltpu.make_async_copy(src, dst, in_sem.at[i])
        for i, (src, dst) in enumerate((
            (v_hbm, v_ext.at[:, 3 : 3 + X, :Y]),
            (f_hbm, f_ext.at[:, 2 : 2 + X, :Y]),
            (r_hbm, r_ext.at[2 : 2 + X, :Y]),
            (m_hbm, m_ref),
        ))
    ]
    for load in loads:
        load.start()

    def exists(axis, high):
        return me[axis] < counts[axis] - 1 if high else me[axis] > 0

    def all_exist(sides, flip):
        there = None
        for axis, high in sides:
            one = exists(axis, high != flip)
            there = one if there is None else there & one
        return there

    def beside(*sides):
        return {axis: me[axis] + (1 if high else -1) for axis, high in sides}

    barrier = pltpu.get_barrier_semaphore()
    expected = blocks - 1
    for step in range(1, blocks):
        pl.semaphore_signal(
            barrier, inc=1, device_id={"gx": lax.rem(me["gx"] + step, blocks)}, device_id_type=MESH
        )
    for sides in around():
        if len(sides) > 1 or sides[0][0] != "gx":
            there = all_exist(sides, False)
            expected = expected + there.astype(jnp.int32)

            @pl.when(there)
            def _():
                pl.semaphore_signal(barrier, inc=1, device_id=beside(*sides), device_id_type=MESH)

    lane = lax.broadcasted_iota(jnp.int32, (8, Z), 1)
    row = lax.broadcasted_iota(jnp.int32, (8, Z), 0)
    place = lane % 8
    group = lane // 8
    low_half = (lane < 32) | (lane >= 96)
    near_groups = (group % 8 == 2) | (group % 8 == 3) | (group % 8 == 4) | (group % 8 == 5)

    def fine_messages(sides):
        at = {axis: high for axis, high in sides}
        x, y, z = at.get("gx"), at.get("gy"), at.get("agg")
        from_x, from_y, from_z = 0 if x else 1, 0 if y else 1, 0 if z else 1
        if z is None and y is None:
            made = []
            for ref, depth, fill in ((v_ext, 3, 0.0), (f_ext, 2, 0.0), (r_ext, 2, far)):
                here = pl.ds(X if x else depth, depth)
                there = pl.ds(0 if x else depth + X, depth)
                index = (slice(None),) if ref is not r_ext else ()
                made.append((ref.at[index + (here, pl.ds(0, Y))], ref.at[index + (there, pl.ds(0, Y))], fill))
            return made
        if z is None and x is None:
            return [(y_send.at[int(y)], y_recv.at[from_y], None)]
        if z is None:
            return [(xy_send.at[2 * int(x) + int(y)], xy_recv.at[2 * from_x + from_y], None)]
        if x is None and y is None:
            return [(z_send, z_recv.at[from_z, :, pl.ds(0, Y)], None)]
        if x is None:
            return [(yz_send.at[int(y)], yz_recv.at[from_z, from_y], None)]
        if y is None:
            return [(xz_send, xz_recv.at[from_z, from_x], None)]
        return [(xz_send.at[0, pl.ds(Y - 8 if y else 0, 8)], corner_recv.at[from_z, from_x, from_y], 0.0)]

    def remote(src, dst, send_sem, recv_sem, sides):
        return pltpu.make_async_remote_copy(
            src_ref=src, dst_ref=dst, send_sem=send_sem, recv_sem=recv_sem,
            device_id=beside(*sides), device_id_type=MESH,
        )

    def fine_copies():
        made, slot = [], 0
        for sides in around():
            for src, dst, _ in fine_messages(sides):
                made.append((sides, remote(src, dst, a_send_sem.at[slot], a_recv_sem.at[slot], sides)))
                slot += 1
        return made

    def start_fine(chosen):
        for sides, copy in fine_copies():
            if chosen(tuple(axis for axis, _ in sides)):
                pl.when(all_exist(sides, False))(copy.start)

    def coarse_message(sides):
        at = {axis: 1 if high else -1 for axis, high in sides}
        block = 1 - at.get("gx", 0)
        here, there = {
            0: (slice(0, Y), slice(0, Y)),
            1: (slice(Y - 8, Y), slice(Y + 8, Y + 16)),
            -1: (slice(0, 8), slice(Y, Y + 8)),
        }[at.get("gy", 0)]
        if "agg" in at:
            return zs_coarse.at[here], h_ext.at[0 if at["agg"] > 0 else 1, block, there]
        return q_ext.at[1, :, here], q_ext.at[block, :, there]

    def coarse_copies():
        return [
            (sides, remote(*coarse_message(sides), q_send_sem.at[slot], q_recv_sem.at[slot], sides))
            for slot, sides in enumerate(around())
        ]

    far_high = jnp.where(low_half, far, 0.0).astype(f32)
    for sides in around():
        @pl.when(jnp.logical_not(all_exist(sides, True)))
        def _():
            axes = tuple(axis for axis, _ in sides)
            for _, target, fill in fine_messages(sides):
                if fill is not None:
                    target[...] = jnp.full(target.shape, fill, f32)
                elif axes == ("gy",):
                    target[: 5 * C] = jnp.zeros((5 * C, 8, Z), f32)
                    target[5 * C :] = jnp.full((2, 8, Z), far, f32)
                elif axes == ("gx", "gy"):
                    target[0:8] = jnp.zeros((8, Z), f32)
                    target[8:16] = jnp.where(row == 4 * C - 8, far, 0.0)
                elif axes == ("agg",):
                    target[:3] = jnp.zeros((3, Y, Z), f32)
                    for t in range(Y // 8):
                        target[3, t * 8 : t * 8 + 8] = far_high
                elif axes == ("gy", "agg"):
                    target[...] = jnp.where(row >= 6, far_high, 0.0)
                else:
                    target[0] = jnp.zeros((Y, Z), f32)
                    for t in range(Y // 8):
                        target[1, t * 8 : t * 8 + 8] = jnp.where(
                            (group == 0) | (group == 1) | (group == 6) | (group == 7), far, 0.0
                        )
            target = coarse_message(sides)[1]
            target[...] = jnp.zeros(target.shape, f32)

    tiles_y = Y // 8
    near, ring = range(tiles_y), range(tiles_y + 1)
    tile_of = lambda t: slice(t * 8, t * 8 + 8)
    even_l = lane % 2 == 0
    even_r = row % 2 == 0
    lane_roll = lambda t, shift: pltpu.roll(t, shift % Z, 1) if shift % Z else t
    row_roll = lambda t, shift: pltpu.roll(t, shift % 8, 0)
    v_flat = v_ext.reshape(C * (X + 6) * rows_ext, Z)
    f_flat = f_ext.reshape(C * (X + 4) * rows_ext, Z)
    r_flat = r_ext.reshape((X + 4) * rows_ext, Z)

    def x_line(number, y):
        if number < 3 * C:
            c, ref, extra = number // 3, v_flat, 3
        elif number < 5 * C:
            c, ref, extra = (number - 3 * C) // 2, f_flat, 2
        else:
            c, ref, extra = 0, r_flat, 2
        return ref, pl.ds((c * (X + 2 * extra) + extra) * rows_ext + y, X, stride=rows_ext)

    depth_of = lambda number: number % 3 if number < 3 * C else (number - 3 * C) % 2

    loads[0].wait()
    loads[1].wait()
    loads[2].wait()
    for number in range(5 * C + 2):
        for side in range(2):
            depth = depth_of(number)
            ref, at = x_line(number, Y - 1 - depth if side else depth)
            y_send[side, number] = ref[at, :]
    for high_x in range(2):
        for high_y in range(2):
            xs = [X - 1 - d if high_x else d for d in range(2)]
            ys = [Y - 1 - d if high_y else d for d in range(2)]
            target = xy_send.at[2 * high_x + high_y]
            for c in range(C):
                for i, (x, y) in enumerate(((xs[0], ys[0]), (xs[1], ys[0]), (xs[0], ys[1]))):
                    target[3 * c + i : 3 * c + i + 1] = v_ext[c, 3 + x, y : y + 1]
                target[3 * C + c : 3 * C + c + 1] = f_ext[c, 2 + xs[0], ys[0] : ys[0] + 1]
            target[4 * C : 4 * C + 1] = r_ext[2 + xs[0], ys[0] : ys[0] + 1]
    pl.semaphore_wait(barrier, expected)
    start_fine(lambda axes: axes == ("gx", "gy"))
    start_fine(lambda axes: axes in (("gx",), ("gy",)))

    v_at = lambda c, x, t: v_ext[c, 3 + x, tile_of(t)]
    f_at = lambda c, x, t: f_ext[c, 2 + x, tile_of(t)]
    held = (
        (lambda x, t: v_at(0, x, t), lambda x, t: v_at(1, x, t)),
        (lambda x, t: v_at(2, x, t), None),
        (lambda x, t: f_at(0, x, t), lambda x, t: f_at(1, x, t)),
        (lambda x, t: f_at(2, x, t), lambda x, t: r_ext[2 + x, tile_of(t)]),
    )
    for t in near:
        turned = []
        for pair in held:
            packed = jnp.zeros((8, Z), f32)
            for half, get in enumerate(pair):
                if get is not None:
                    for x in range(X):
                        at = (x + 4 + 8 * half) % 16
                        packed = jnp.where(group == at, lane_roll(get(x, t), 8 * at + 3), packed)
            out = jnp.where(place == 3, packed, lane_roll(packed, 6))
            for spot, shift in ((2, -2), (1, -4), (4, 2), (5, 4)):
                out = jnp.where(place == spot, lane_roll(packed, shift), out)
            turned.append(out)
        for i in range(4):
            z_send[i, tile_of(t)] = turned[i]
            for side in range(2):
                if t == (tiles_y - 1 if side else 0):
                    first = 6 if side else 0
                    yz_send[side, 2 * i : 2 * i + 2] = turned[i][first : first + 2]
        for i in range(2):
            xz_send[i, tile_of(t)] = jnp.where(near_groups, turned[2 * i], lane_roll(turned[2 * i + 1], 32))
    start_fine(lambda axes: axes == ("gx", "gy", "agg"))
    start_fine(lambda axes: axes in (("gx", "agg"), ("gy", "agg")))
    start_fine(lambda axes: axes == ("agg",))

    kept = X // 2
    parts = Y // 8
    combos_per_tile = Z // chunk

    def c_copy(j, source):
        return pltpu.make_async_remote_copy(
            src_ref=c_send.at[j],
            dst_ref=c_recv.at[source],
            send_sem=c_send_sem.at[j],
            recv_sem=c_recv_sem.at[source],
            device_id={"gx": j},
            device_id_type=MESH,
        )

    def finish_compressed(tiles):
        coefs = blocks * kept
        for tile in tiles:
            gathered = c_recv[:, tile].reshape(coefs * 8, Z)
            done = lax.dot_general(
                m_ref[...], gathered, (((1,), (0,)), ((), ())),
                precision=lax.Precision.HIGHEST, preferred_element_type=jnp.float32,
            )
            for place in range(combos_per_tile):
                c, part = divmod(tile * combos_per_tile + place, parts)
                if c < C:
                    for y in range(8):
                        comp_ref[c, part * 8 + y] = done[
                            y * coefs : (y + 1) * coefs, place * chunk : (place + 1) * chunk
                        ]

    lane_swap = lambda t: jnp.where(even_l, lane_roll(t, -1), lane_roll(t, 1))
    row_swap = lambda t: jnp.where(even_r, row_roll(t, -1), row_roll(t, 1))
    slot_at = lane % 16
    corner_of = ((0, 0), (0, 1), (1, 1), (1, 0))

    def pooled(planes):
        pairs = [[planes[x][t] + planes[x + 1][t] for t in near] for x in range(0, X, 2)]
        out = []
        for t in near:
            t0, t1, t2, t3 = (pair[t] for pair in pairs)
            left = jnp.where(even_r, t0, t3) + row_swap(jnp.where(even_r, t3, t0))
            right = jnp.where(even_r, t1, t2) + row_swap(jnp.where(even_r, t2, t1))
            out.append(jnp.where(even_l, left, right) + lane_swap(jnp.where(even_l, right, left)))
        return out

    def edge_lanes(fields, t):
        packed = jnp.zeros((8, Z), f32)
        for start, field in fields:
            for depth in range(1, 5):
                high = (lane >= start + 8 - 2 * depth) & (lane < start + 10 - 2 * depth)
                packed = jnp.where(high, lane_roll(field[t], start + 10 - 4 * depth), packed)
                low = (lane >= start + 6 + 2 * depth) & (lane < start + 8 + 2 * depth)
                packed = jnp.where(low, lane_roll(field[t], start + 6 + 4 * depth), packed)
        return packed

    coarse_weight = [
        damping / ((6.0 + 0.5 * total) * 0.25)
        for total in pooled([[r_ext[2 + x, tile_of(t)] for t in near] for x in range(X)])
    ]
    coarse_step = [0.25 * weight for weight in coarse_weight]
    step_edges = [edge_lanes([(64 + 16 * c, coarse_step) for c in range(C)], t) for t in near]
    for t in near:
        q_ext[1, C, tile_of(t)] = coarse_step[t]
        zs_coarse[tile_of(t)] = step_edges[t]
    for x in range(X):
        for t in near:
            w_ext[2 + x, tile_of(t)] = damping / (6.0 + r_ext[2 + x, tile_of(t)])

    levels = local_levels(X)
    for c in range(C):
        for t in near:
            approx, details = [v_at(c, x, t) for x in range(X)], []
            for level in range(levels):
                low, high = approx[0::2], approx[1::2]
                approx = [(a + b) * root_half for a, b in zip(low, high)]
                if level > 0:
                    details = [(a - b) * root_half for a, b in zip(low, high)] + details
            tile, spot = divmod(c * parts + t, combos_per_tile)
            inside = (lane >= spot * chunk) & (lane < (spot + 1) * chunk)
            for k, values in enumerate(approx + details):
                done = (jnp.where(even_l, values, -values) + lane_swap(values)) * root_half
                for j in range(blocks):
                    moved = lane_roll(done, spot * chunk - j * chunk)
                    if spot:
                        moved = jnp.where(inside, moved, c_send[j, tile, k])
                    c_send[j, tile, k] = moved

    for sides, copy in fine_copies():
        pl.when(all_exist(sides, True))(copy.wait_recv)

    for j in range(blocks):
        pl.when(me["gx"] != j)(c_copy(j, me["gx"]).start)

    for number in range(5 * C + 2):
        for side in range(2):
            depth = depth_of(number)
            ref, at = x_line(number, Y + depth if side else rows_ext - 1 - depth)
            ref[at, :] = y_recv[side, number]
    for high_x in range(2):
        for high_y in range(2):
            xs = [X + d if high_x else -1 - d for d in range(2)]
            ys = [Y + d if high_y else rows_ext - 1 - d for d in range(2)]
            source = xy_recv.at[2 * high_x + high_y]
            for c in range(C):
                for i, (x, y) in enumerate(((xs[0], ys[0]), (xs[1], ys[0]), (xs[0], ys[1]))):
                    v_ext[c, 3 + x, y : y + 1] = source[3 * c + i : 3 * c + i + 1]
                f_ext[c, 2 + xs[0], ys[0] : ys[0] + 1] = source[3 * C + c : 3 * C + c + 1]
            r_ext[2 + xs[0], ys[0] : ys[0] + 1] = source[4 * C : 4 * C + 1]
    for side in range(2):
        for i in range(4):
            z_recv[side, i, Y : Y + 2] = yz_recv[side, 1, 2 * i : 2 * i + 2]
            z_recv[side, i, Y + 6 : Y + 8] = yz_recv[side, 0, 2 * i : 2 * i + 2]

    def weight_of(reaction):
        return jnp.where(reaction < 0.1 * far, damping / (6.0 + reaction), 0.0)

    for x in range(-2, X + 2):
        outside = max(-x, x - X + 1)
        for t in ring:
            if (outside > 0 and t < tiles_y) or (t == tiles_y and outside < 2):
                w_ext[2 + x, tile_of(t)] = weight_of(r_ext[2 + x, tile_of(t)])

    mixed = {}
    for i in range(4):
        for t in ring:
            mixed[i, t] = jnp.where(place < 4, z_recv[1, i, tile_of(t)], z_recv[0, i, tile_of(t)])
    beyond = {}
    for side in range(2):
        for i in range(2):
            for t in near:
                beyond[side, i, t] = jnp.where(
                    place < 4, xz_recv[1, side, i, tile_of(t)], xz_recv[0, side, i, tile_of(t)]
                )
        ends = [
            jnp.where(place < 4, corner_recv[1, side, high], corner_recv[0, side, high]) for high in range(2)
        ]
        beyond[side, 0, tiles_y] = jnp.where(row < 4, ends[1], ends[0])

    def edge_field(number, t):
        i, half = divmod(number, 2)
        value = lane_roll(mixed[i, t], 64 * half)
        if t < tiles_y or number < 4:
            shift = (64, 0, 32, -32)[number % 4]
            low, high = (lane_roll(beyond[side, i // 2, t], shift) for side in range(2))
            value = jnp.where(group < 4, low, jnp.where(group >= 12, high, value))
        return value

    edge_v = {(c, t): edge_field(c, t) for c in range(C) for t in ring}
    edge_f = {(c, t): edge_field(4 + c, t) for c in range(C) for t in ring}
    edge_w = {t: weight_of(edge_field(7, t)) for t in ring}

    def around_rows(get, t, tiles, by):
        after, before = (t + 1) % tiles, (t - 1) % tiles
        own = get(t)
        above = jnp.where(row < 8 - by, row_roll(own, -by), row_roll(get(after), -by))
        below = jnp.where(row >= by, row_roll(own, by), row_roll(get(before), by))
        return below, above

    def main_total(get, edge, c, x, t):
        below, above = around_rows(lambda t: get(c, x, t), t, tiles_y + 1, 1)
        total = (get(c, x - 1, t) + get(c, x + 1, t)) + (below + above)
        beside_z = lane_roll(edge[c, t], -(8 * (x + 4) + 4))
        own = get(c, x, t)
        total = total + jnp.where(lane == 0, beside_z, lane_roll(own, 1))
        return total + jnp.where(lane == Z - 1, beside_z, lane_roll(own, -1))

    def edge_total(get, edge, c, xs, t):
        own = edge[c, t]
        line = own
        for x in xs:
            line = jnp.where(group == x + 4, lane_roll(get(c, x, t), 8 * (x + 4) + 4), line)
        below, above = around_rows(lambda t: edge[c, t], t, tiles_y + 1, 1)
        total = (lane_roll(own, 8) + lane_roll(own, -8)) + (below + above)
        total = total + jnp.where(place == 4, line, lane_roll(own, 1))
        return total + jnp.where(place == 3, line, lane_roll(own, -1))

    u1_at = lambda c, x, t: u1_ext[c, 2 + x, tile_of(t)]
    u2_at = lambda c, x, t: u2_ext[c, 1 + x, tile_of(t)]
    w_at = lambda x, t: w_ext[2 + x, tile_of(t)]

    edge_1, edge_2 = {}, {}
    for c in range(C):
        for t in ring:
            total = edge_total(v_at, edge_v, c, range(-1, X + 1), t)
            edge_1[c, t] = keep * edge_v[c, t] + edge_w[t] * (edge_f[c, t] + total)
        for x in range(-2, X + 2):
            for t in near if x in (-2, X + 1) else ring:
                total = main_total(v_at, edge_v, c, x, t)
                u1_ext[c, 2 + x, tile_of(t)] = keep * v_at(c, x, t) + w_at(x, t) * (f_at(c, x, t) + total)
    for c in range(C):
        for t in near:
            total = edge_total(u1_at, edge_1, c, range(X), t)
            edge_2[c, t] = keep * edge_1[c, t] + edge_w[t] * (edge_f[c, t] + total)
        for x in range(-1, X + 1):
            for t in near if x in (-1, X) else ring:
                total = main_total(u1_at, edge_1, c, x, t)
                u2_ext[c, 1 + x, tile_of(t)] = keep * u1_at(c, x, t) + w_at(x, t) * (f_at(c, x, t) + total)
    sums = [
        [[main_total(u2_at, edge_2, c, x, t) + f_at(c, x, t) for t in near] for x in range(X)] for c in range(C)
    ]

    correction = []
    for c in range(C):
        rhs = pooled([
            [sums[c][x][t] - (6.0 + r_ext[2 + x, tile_of(t)]) * u2_at(c, x, t) for t in near] for x in range(X)
        ])
        correction.append([weight * (0.125 * total) for weight, total in zip(coarse_weight, rhs)])
    for c in range(C):
        for t in near:
            q_ext[1, c, tile_of(t)] = correction[c][t]
    for t in near:
        edges_t = edge_lanes([(16 * c, correction[c]) for c in range(C)], t)
        zs_coarse[tile_of(t)] = jnp.where(lane < 64, edges_t, zs_coarse[tile_of(t)])
    for sides, copy in coarse_copies():
        pl.when(all_exist(sides, False))(copy.start)

    for j in range(blocks):
        @pl.when(me["gx"] == j)
        def _():
            c_recv[j] = c_send[j]

    for j in range(blocks):
        pl.when(me["gx"] != j)(c_copy(j, j).wait_recv)
    loads[3].wait()
    finish_compressed(range(c_send.shape[1]))

    for sides, copy in coarse_copies():
        pl.when(all_exist(sides, True))(copy.wait_recv)

    ring = range(tiles_y + 2)
    after = lambda t: (t + 1) % len(ring)
    before = lambda t: (t - 1) % len(ring)
    main = {(b, c, t): q_ext[b, c, tile_of(t)] for b in range(3) for c in range(C) for t in ring}
    step_main = {(b, t): q_ext[b, C, tile_of(t)] for b in range(3) for t in ring}
    edge = {
        (b, t): jnp.where(slot_at < 8, h_ext[1, b, tile_of(t)], h_ext[0, b, tile_of(t)])
        for b in range(3) for t in ring
    }
    step_edge = {key: lane_roll(value, -64) for key, value in edge.items()}
    first_main, first_edge = dict(main), dict(edge)

    def above(get, t):
        return jnp.where(row < 6, row_roll(get(t), -2), row_roll(get(after(t)), -2))

    def below(get, t):
        return jnp.where(row >= 2, row_roll(get(t), 2), row_roll(get(before(t)), 2))

    def along(get, b, t):
        low, high = get(max(b - 1, 0), t), get(min(b + 1, 2), t)
        across = jnp.where(even_l, jnp.where(even_r, high, low), get(b, t))
        return lane_swap(get(b, t)) + row_swap(across)

    def inject(edge, b, c, t):
        return lane_roll(edge[b, t], -(16 * c + 8))

    def left_of(main, edge, b, c, t):
        return jnp.where(lane < 2, inject(edge, b, c, t), lane_roll(main[b, c, t], 2))

    def right_of(main, edge, b, c, t):
        return jnp.where(lane >= Z - 2, inject(edge, b, c, t), lane_roll(main[b, c, t], -2))

    def coarse_sweep(main, edge, main_at, edge_at):
        new_main, new_edge = dict(main), dict(edge)
        for b, t in main_at:
            for c in range(C):
                get = lambda b, t, c=c: main[b, c, t]
                row_get = lambda t, b=b, c=c: main[b, c, t]
                total = along(get, b, t) + (above(row_get, t) + below(row_get, t))
                total = total + (left_of(main, edge, b, c, t) + right_of(main, edge, b, c, t))
                new_main[b, c, t] = keep * main[b, c, t] + first_main[b, c, t] + step_main[b, t] * total
        for b, t in edge_at:
            get = lambda b, t: edge[b, t]
            row_get = lambda t, b=b: edge[b, t]
            own = lane_roll(main[b, 0, t], 8)
            for c in range(1, C):
                own = jnp.where(lane < 16 * c, own, lane_roll(main[b, c, t], 16 * c + 8))
            total = along(get, b, t) + (above(row_get, t) + below(row_get, t))
            total = total + jnp.where((slot_at == 8) | (slot_at == 9), own, lane_roll(edge[b, t], 2))
            total = total + jnp.where((slot_at == 6) | (slot_at == 7), own, lane_roll(edge[b, t], -2))
            new_edge[b, t] = keep * edge[b, t] + first_edge[b, t] + step_edge[b, t] * total
        return new_main, new_edge

    everywhere = [(b, t) for b in range(3) for t in ring]
    centre = [(1, t) for t in ring]
    sides_near = [(b, t) for b in (0, 2) for t in near]
    main, edge = coarse_sweep(main, edge, everywhere, everywhere)
    main, edge = coarse_sweep(main, edge, everywhere, centre + sides_near)
    main, edge = coarse_sweep(main, edge, centre + sides_near, [(1, t) for t in near])

    def spread_rows(even, odd, pa):
        if pa == 0:
            return jnp.where(even_r, even, row_roll(odd, 1))
        return jnp.where(even_r, row_roll(even, -1), odd)

    def spread_lanes(even, odd, pb):
        if pb == 0:
            return jnp.where(even_l, even, lane_roll(odd, 1))
        return jnp.where(even_l, lane_roll(even, -1), odd)

    for c in range(C):
        for t in near:
            at = tile_of(t)
            row_get = lambda t, c=c: main[1, c, t]
            own = main[1, c, t]
            rows_near = (below(row_get, t), above(row_get, t))
            lanes_near = (left_of(main, edge, 1, c, t), right_of(main, edge, 1, c, t))
            alone = [spread_lanes(own, own, pb) for pb in range(2)]
            spread = [spread_rows(alone[pb], alone[pb], pa) for pa, pb in corner_of]
            low, high = (spread_lanes(main[b, c, t], main[b, c, t], 0) for b in (0, 2))
            spread = [spread_rows(low, low, 1)] + spread + [spread_rows(high, high, 0)]
            based = [3.0 * own + rows_near[a] for a in range(2)]
            wide = [
                [spread_lanes(based[a] + lanes_near[0], based[a] + lanes_near[1], pb) for pb in range(2)]
                for a in range(2)
            ]
            for x in range(X):
                p = x // 2
                pa, pb = corner_of[p]
                added = spread_rows(wide[0][pb], wide[1][pb], pa) + spread[p + 2 * (x % 2)]
                total = sums[c][x][t] + added
                vel_ref[c, x, at] = keep * (u2_at(c, x, t) + spread[p + 1]) + w_at(x, t) * total

    for sides, copy in fine_copies():
        pl.when(all_exist(sides, False))(copy.wait_send)
    for sides, copy in coarse_copies():
        pl.when(all_exist(sides, False))(copy.wait_send)
    for j in range(blocks):
        pl.when(me["gx"] != j)(c_copy(j, me["gx"]).wait_send)


def on_device(counts, velocity_prev, forcing, reaction):
    C, X, Y, Z = velocity_prev.shape
    blocks = counts["gx"]
    kept = X // 2
    chunk = Z // blocks
    tiles = -(-(C * (Y // 8)) // (Z // chunk))
    matrix = jnp.asarray(finish_matrix(X, blocks, 8))
    vmem = pl.BlockSpec(memory_space=pltpu.VMEM)
    space = lambda *shape: pltpu.VMEM(shape, jnp.float32)

    velocity, compressed = pl.pallas_call(
        functools.partial(kernel, counts),
        out_shape=(
            jax.ShapeDtypeStruct((C, X, Y, Z), jnp.float32),
            jax.ShapeDtypeStruct((C, Y, kept * blocks, chunk), jnp.float32),
        ),
        in_specs=[pl.BlockSpec(memory_space=pltpu.HBM)] * 4,
        out_specs=(vmem, vmem),
        scratch_shapes=[
            space(C, X + 6, Y + 8, Z),
            space(C, X + 4, Y + 8, Z),
            space(X + 4, Y + 8, Z),
            space(*matrix.shape),
            space(X + 4, Y + 8, Z),
            space(C, X + 4, Y + 8, Z),
            space(C, X + 2, Y + 8, Z),
            space(2, 5 * C + 2, X, Z),
            space(2, 5 * C + 2, X, Z),
            space(4, 16, Z),
            space(4, 16, Z),
            space(4, Y, Z),
            space(2, 4, Y + 8, Z),
            space(2, 8, Z),
            space(2, 2, 8, Z),
            space(2, Y, Z),
            space(2, 2, 2, Y, Z),
            space(2, 2, 2, 8, Z),
            space(3, C + 1, Y + 16, Z),
            space(2, 3, Y + 16, Z),
            space(Y, Z),
            space(blocks, tiles, kept, 8, Z),
            space(blocks, tiles, kept, 8, Z),
            pltpu.SemaphoreType.DMA((30,)),
            pltpu.SemaphoreType.DMA((30,)),
            pltpu.SemaphoreType.DMA((26,)),
            pltpu.SemaphoreType.DMA((26,)),
            pltpu.SemaphoreType.DMA((blocks,)),
            pltpu.SemaphoreType.DMA((blocks,)),
            pltpu.SemaphoreType.DMA((4,)),
        ],
        compiler_params=pltpu.CompilerParams(collective_id=0, has_side_effects=True, vmem_limit_bytes=40000000),
    )(*(pltpu.with_memory_space_constraint(a, pltpu.HBM) for a in (velocity_prev, forcing, reaction, matrix)))
    return velocity, jnp.swapaxes(compressed, 2, 3)


def solution(mesh):
    counts = {axis: mesh.shape[axis] for axis in ("agg", "gx", "gy")}
    placed = (P(None, "gx", "gy", "agg"), P(None, "gx", "gy", "agg"), P("gx", "gy", "agg"))
    return jax.shard_map(
        functools.partial(on_device, counts),
        mesh=mesh,
        in_specs=placed,
        out_specs=(P(None, "gx", "gy", "agg"), P(None, "gy", ("agg", "gx"), None)),
        check_vma=False,
    )
```

time: 20.7 us -> 19.2 us (0.928)
  Pallas kernels: 18.5 us -> 17 us
    pallas_call x1, Pallas kernels: 18.5 us -> 17 us  [on_device(): pl.pallas_call(functools.partial(kernel, counts), out_shape=(jax.ShapeDty...]
where the time goes in v2:
time: 19.2 us; the launch traced here: 19 us
  Pallas kernels  17 us (89%)
  local copies, waits for them, and re-layouts  1.42 us (7%)
  between operations  0.64 us (3%)
    pallas_call x1, Pallas kernels, on_device(): pl.pallas_call(functools.partial(kernel, counts), out_shape=(jax.ShapeDty...  17 us
    unnamed x2, local copies, waits for them, and re-layouts  1.42 us

profile of v2, /device:TPU:0, one launch (start us, length us, event | category | flops | bytes accessed | tf_op | source)
XLA Modules:
  0.0 19.0 jit_solution(16647051947876347543)
XLA Ops:
  0.6 17.0 %shard_map.59 = (f32[3,8,16,128]{3,2,1,0:T(8,128)S(1)}, f32[3,16,16,32]{3,2,1,0:T(8,128)S(1)}) custom-call(f32[3,8,16,128]{3,2,1,0:T(8,128)} %v_hbm.1, f32[3,8,16,128]{3,2,1,0:T(8,128)} %f_hbm.1, f32[8,16,128]{2,1,0:T(8,128)} %r_hbm.1, f32[128,128]{1,0:T(8,128)} %constant.2.clone.m_hbm), custom_call_target="tpu_custom_call" | custom-call | tf_op jit(solution)/shard_map/pallas_call | solution.py:628
  17.6 0.7 %copy.8 = f32[3,8,16,128]{3,2,1,0:T(8,128)} copy(f32[3,8,16,128]{3,2,1,0:T(8,128)S(1)} %get-tuple-element.8) | data formatting | bytes 393216
  18.3 0.7 %copy.9 = f32[3,16,32,16]{2,3,1,0:T(8,128)} copy(f32[3,16,32,16]{2,3,1,0:T(8,128)S(1)} %bitcast.1) | data formatting | bytes 196608

commit v3 on v2

--- a/solution.py
+++ b/solution.py
@@ -1,4 +1,6 @@
 import functools
+import itertools
+import math
 
 import jax
 import jax.numpy as jnp
@@ -60,7 +62,7 @@
 def kernel(
     sizes, v_hbm, f_hbm, r_hbm, m_hbm, vel_ref, comp_ref, v_ext, f_ext, r_ext, m_ref, w_ext, u1_ext, u2_ext,
     y_send, y_recv, xy_send, xy_recv, z_send, z_recv, yz_send, yz_recv, xz_send, xz_recv, corner_recv,
-    q_ext, h_ext, zs_coarse, c_send, c_recv,
+    q_ext, h_ext, zs_coarse, c_send, c_recv, measure,
     a_send_sem, a_recv_sem, q_send_sem, q_recv_sem, c_send_sem, c_recv_sem, in_sem,
 ):
     counts = sizes
@@ -98,18 +100,19 @@
 
     barrier = pltpu.get_barrier_semaphore()
     expected = blocks - 1
+    for sides in around():
+        if len(sides) > 1 or sides[0][0] != "gx":
+            there = all_exist(sides, False)
+            expected = expected + there.astype(jnp.int32)
+
+            @pl.when(there)
+            def _():
+                pl.semaphore_signal(barrier, inc=1, device_id=beside(*sides), device_id_type=MESH)
+
     for step in range(1, blocks):
         pl.semaphore_signal(
             barrier, inc=1, device_id={"gx": lax.rem(me["gx"] + step, blocks)}, device_id_type=MESH
         )
-    for sides in around():
-        if len(sides) > 1 or sides[0][0] != "gx":
-            there = all_exist(sides, False)
-            expected = expected + there.astype(jnp.int32)
-
-            @pl.when(there)
-            def _():
-                pl.semaphore_signal(barrier, inc=1, device_id=beside(*sides), device_id_type=MESH)
 
     lane = lax.broadcasted_iota(jnp.int32, (8, Z), 1)
     row = lax.broadcasted_iota(jnp.int32, (8, Z), 0)
@@ -149,19 +152,38 @@
         )
 
     def fine_copies():
-        made, slot = [], 0
-        for sides in around():
-            for src, dst, _ in fine_messages(sides):
-                made.append((sides, remote(src, dst, a_send_sem.at[slot], a_recv_sem.at[slot], sides)))
-                slot += 1
-        return made
-
-    def start_fine(chosen):
-        for sides, copy in fine_copies():
-            if chosen(tuple(axis for axis, _ in sides)):
-                pl.when(all_exist(sides, False))(copy.start)
-
-    def coarse_message(sides):
+        return [
+            (sides, remote(src, dst, a_send_sem.at[0], a_recv_sem.at[0], sides))
+            for sides in around()
+            for src, dst, _ in fine_messages(sides)
+        ]
+
+    def rows_of(copies):
+        found = {}
+        for sides, copy in copies:
+            axes = tuple(axis for axis, _ in sides)
+            if all(high for _, high in sides):
+                found[axes] = found.get(axes, 0) + math.prod(copy.src_ref.shape[:-1])
+        return found
+
+    def settle(copies, sem):
+        sizes = rows_of(copies)
+        neighbours = {
+            axis: exists(axis, False).astype(jnp.int32) + exists(axis, True).astype(jnp.int32) for axis in counts
+        }
+        options = {axis: {1: (0,), 2: (1,)}.get(count, (1, 2)) for axis, count in counts.items()}
+        for numbers in itertools.product(*options.values()):
+            number = dict(zip(options, numbers))
+            rows = sum(size * math.prod(number[axis] for axis in axes) for axes, size in sizes.items())
+            there = None
+            for axis, value in number.items():
+                one = neighbours[axis] == value
+                there = one if there is None else there & one
+            if rows:
+                part = measure.at[pl.ds(0, rows)]
+                pl.when(there)(pltpu.make_async_copy(part, part, sem).wait)
+
+    def coarse_message(sides, first=0, fields=C):
         at = {axis: 1 if high else -1 for axis, high in sides}
         block = 1 - at.get("gx", 0)
         here, there = {
@@ -171,12 +193,20 @@
         }[at.get("gy", 0)]
         if "agg" in at:
             return zs_coarse.at[here], h_ext.at[0 if at["agg"] > 0 else 1, block, there]
-        return q_ext.at[1, :, here], q_ext.at[block, :, there]
+        which = pl.ds(first, fields)
+        return q_ext.at[1, which, here], q_ext.at[block, which, there]
 
     def coarse_copies():
         return [
-            (sides, remote(*coarse_message(sides), q_send_sem.at[slot], q_recv_sem.at[slot], sides))
-            for slot, sides in enumerate(around())
+            (sides, remote(*coarse_message(sides), q_send_sem.at[0], q_recv_sem.at[0], sides))
+            for sides in around()
+        ]
+
+    def step_copies():
+        return [
+            (sides, remote(*coarse_message(sides, C, 1), q_send_sem.at[1], q_recv_sem.at[1], sides))
+            for sides in around()
+            if "agg" not in dict(sides)
         ]
 
     far_high = jnp.where(low_half, far, 0.0).astype(f32)
@@ -205,8 +235,8 @@
                         target[1, t * 8 : t * 8 + 8] = jnp.where(
                             (group == 0) | (group == 1) | (group == 6) | (group == 7), far, 0.0
                         )
-            target = coarse_message(sides)[1]
-            target[...] = jnp.zeros(target.shape, f32)
+            for target in [coarse_message(sides)[1], coarse_message(sides, C, 1)[1]][: 1 + ("agg" not in axes)]:
+                target[...] = jnp.zeros(target.shape, f32)
 
     tiles_y = Y // 8
     near, ring = range(tiles_y), range(tiles_y + 1)
@@ -248,10 +278,6 @@
                     target[3 * c + i : 3 * c + i + 1] = v_ext[c, 3 + x, y : y + 1]
                 target[3 * C + c : 3 * C + c + 1] = f_ext[c, 2 + xs[0], ys[0] : ys[0] + 1]
             target[4 * C : 4 * C + 1] = r_ext[2 + xs[0], ys[0] : ys[0] + 1]
-    pl.semaphore_wait(barrier, expected)
-    start_fine(lambda axes: axes == ("gx", "gy"))
-    start_fine(lambda axes: axes in (("gx",), ("gy",)))
-
     v_at = lambda c, x, t: v_ext[c, 3 + x, tile_of(t)]
     f_at = lambda c, x, t: f_ext[c, 2 + x, tile_of(t)]
     held = (
@@ -281,9 +307,9 @@
                     yz_send[side, 2 * i : 2 * i + 2] = turned[i][first : first + 2]
         for i in range(2):
             xz_send[i, tile_of(t)] = jnp.where(near_groups, turned[2 * i], lane_roll(turned[2 * i + 1], 32))
-    start_fine(lambda axes: axes == ("gx", "gy", "agg"))
-    start_fine(lambda axes: axes in (("gx", "agg"), ("gy", "agg")))
-    start_fine(lambda axes: axes == ("agg",))
+    pl.semaphore_wait(barrier, expected)
+    for sides, copy in fine_copies():
+        pl.when(all_exist(sides, False))(copy.start)
 
     kept = X // 2
     parts = Y // 8
@@ -293,11 +319,17 @@
         return pltpu.make_async_remote_copy(
             src_ref=c_send.at[j],
             dst_ref=c_recv.at[source],
-            send_sem=c_send_sem.at[j],
-            recv_sem=c_recv_sem.at[source],
+            send_sem=c_send_sem.at[0],
+            recv_sem=c_recv_sem.at[0],
             device_id={"gx": j},
             device_id_type=MESH,
         )
+
+    def settle_parts(sem):
+        rows = (blocks - 1) * math.prod(c_send.shape[1:-1])
+        if rows:
+            part = measure.at[pl.ds(0, rows)]
+            pltpu.make_async_copy(part, part, sem).wait()
 
     def finish_compressed(tiles):
         coefs = blocks * kept
@@ -372,9 +404,10 @@
                         moved = jnp.where(inside, moved, c_send[j, tile, k])
                     c_send[j, tile, k] = moved
 
-    for sides, copy in fine_copies():
-        pl.when(all_exist(sides, True))(copy.wait_recv)
-
+    settle(fine_copies(), a_recv_sem.at[0])
+
+    for sides, copy in step_copies():
+        pl.when(all_exist(sides, False))(copy.start)
     for j in range(blocks):
         pl.when(me["gx"] != j)(c_copy(j, me["gx"]).start)
 
@@ -506,13 +539,12 @@
         def _():
             c_recv[j] = c_send[j]
 
-    for j in range(blocks):
-        pl.when(me["gx"] != j)(c_copy(j, j).wait_recv)
+    settle_parts(c_recv_sem.at[0])
     loads[3].wait()
     finish_compressed(range(c_send.shape[1]))
 
-    for sides, copy in coarse_copies():
-        pl.when(all_exist(sides, True))(copy.wait_recv)
+    settle(step_copies(), q_recv_sem.at[1])
+    settle(coarse_copies(), q_recv_sem.at[0])
 
     ring = range(tiles_y + 2)
     after = lambda t: (t + 1) % len(ring)
@@ -607,12 +639,10 @@
                 total = sums[c][x][t] + added
                 vel_ref[c, x, at] = keep * (u2_at(c, x, t) + spread[p + 1]) + w_at(x, t) * total
 
-    for sides, copy in fine_copies():
-        pl.when(all_exist(sides, False))(copy.wait_send)
-    for sides, copy in coarse_copies():
-        pl.when(all_exist(sides, False))(copy.wait_send)
-    for j in range(blocks):
-        pl.when(me["gx"] != j)(c_copy(j, me["gx"]).wait_send)
+    settle(fine_copies(), a_send_sem.at[0])
+    settle(step_copies(), q_send_sem.at[1])
+    settle(coarse_copies(), q_send_sem.at[0])
+    settle_parts(c_send_sem.at[0])
 
 
 def on_device(counts, velocity_prev, forcing, reaction):
@@ -657,12 +687,13 @@
             space(Y, Z),
             space(blocks, tiles, kept, 8, Z),
             space(blocks, tiles, kept, 8, Z),
-            pltpu.SemaphoreType.DMA((30,)),
-            pltpu.SemaphoreType.DMA((30,)),
-            pltpu.SemaphoreType.DMA((26,)),
-            pltpu.SemaphoreType.DMA((26,)),
-            pltpu.SemaphoreType.DMA((blocks,)),
-            pltpu.SemaphoreType.DMA((blocks,)),
+            space(max((blocks - 1) * tiles * kept * 8, 128 * Y), Z),
+            pltpu.SemaphoreType.DMA((1,)),
+            pltpu.SemaphoreType.DMA((1,)),
+            pltpu.SemaphoreType.DMA((2,)),
+            pltpu.SemaphoreType.DMA((2,)),
+            pltpu.SemaphoreType.DMA((1,)),
+            pltpu.SemaphoreType.DMA((1,)),
             pltpu.SemaphoreType.DMA((4,)),
         ],
         compiler_params=pltpu.CompilerParams(collective_id=0, has_side_effects=True, vmem_limit_bytes=40000000),

time: 19.2 us -> 16.9 us (0.88)
  Pallas kernels: 17 us -> 14.7 us
    pallas_call x1, Pallas kernels: 17 us -> 14.7 us  [on_device(): pl.pallas_call(functools.partial(kernel, counts), out_shape=(jax.ShapeDty...]
where the time goes in v3:
time: 16.9 us; the launch traced here: 16.8 us
  Pallas kernels  14.7 us (87%)
  local copies, waits for them, and re-layouts  1.42 us (8%)
  between operations  0.64 us (4%)
    pallas_call x1, Pallas kernels, on_device(): pl.pallas_call(functools.partial(kernel, counts), out_shape=(jax.ShapeDty...  14.7 us
    unnamed x2, local copies, waits for them, and re-layouts  1.42 us

profile of v3, /device:TPU:0, one launch (start us, length us, event | category | flops | bytes accessed | tf_op | source)
XLA Modules:
  0.0 16.8 jit_solution(11354701591479911591)
XLA Ops:
  0.6 14.7 %shard_map.59 = (f32[3,8,16,128]{3,2,1,0:T(8,128)S(1)}, f32[3,16,16,32]{3,2,1,0:T(8,128)S(1)}) custom-call(f32[3,8,16,128]{3,2,1,0:T(8,128)} %v_hbm.1, f32[3,8,16,128]{3,2,1,0:T(8,128)} %f_hbm.1, f32[8,16,128]{2,1,0:T(8,128)} %r_hbm.1, f32[128,128]{1,0:T(8,128)} %constant.2.clone.m_hbm), custom_call_target="tpu_custom_call" | custom-call | tf_op jit(solution)/shard_map/pallas_call | solution.py:658
  15.4 0.7 %copy.8 = f32[3,8,16,128]{3,2,1,0:T(8,128)} copy(f32[3,8,16,128]{3,2,1,0:T(8,128)S(1)} %get-tuple-element.8) | data formatting | bytes 393216
  16.0 0.7 %copy.9 = f32[3,16,32,16]{2,3,1,0:T(8,128)} copy(f32[3,16,32,16]{2,3,1,0:T(8,128)S(1)} %bitcast.1) | data formatting | bytes 196608

commit v4 on v3

--- a/solution.py
+++ b/solution.py
@@ -645,6 +645,17 @@
     settle_parts(c_send_sem.at[0])
 
 
+def write_out(vel_ref, comp_ref, vel_hbm, comp_hbm, sem):
+    copies = [
+        pltpu.make_async_copy(comp_ref, comp_hbm, sem.at[0]),
+        pltpu.make_async_copy(vel_ref, vel_hbm, sem.at[1]),
+    ]
+    for copy in copies:
+        copy.start()
+    for copy in copies:
+        copy.wait()
+
+
 def on_device(counts, velocity_prev, forcing, reaction):
     C, X, Y, Z = velocity_prev.shape
     blocks = counts["gx"]
@@ -698,6 +709,17 @@
         ],
         compiler_params=pltpu.CompilerParams(collective_id=0, has_side_effects=True, vmem_limit_bytes=40000000),
     )(*(pltpu.with_memory_space_constraint(a, pltpu.HBM) for a in (velocity_prev, forcing, reaction, matrix)))
+    velocity, compressed = pl.pallas_call(
+        write_out,
+        out_shape=(
+            jax.ShapeDtypeStruct(velocity.shape, jnp.float32),
+            jax.ShapeDtypeStruct(compressed.shape, jnp.float32),
+        ),
+        in_specs=[vmem, vmem],
+        out_specs=[pl.BlockSpec(memory_space=pltpu.HBM)] * 2,
+        scratch_shapes=[pltpu.SemaphoreType.DMA((2,))],
+        compiler_params=pltpu.CompilerParams(vmem_limit_bytes=4000000),
+    )(velocity, compressed)
     return velocity, jnp.swapaxes(compressed, 2, 3)
 
 

time: 16.9 us -> 16.3 us (0.964)
  local copies, waits for them, and re-layouts: 1.42 us -> 0 us
  Pallas kernels: 14.7 us -> 15.5 us
    unnamed x2 -> x0, local copies, waits for them, and re-layouts: 1.42 us -> none
    pallas_call x0 -> x1, Pallas kernels: none -> 0.83 us  [on_device(): pl.pallas_call(write_out, out_shape=(jax.ShapeDtypeStruct(velocity.shape,...]
where the time goes in v4:
time: 16.3 us; the launch traced here: 16.2 us
  Pallas kernels  15.5 us (95%)
  between operations  0.64 us (4%)
    pallas_call x1, Pallas kernels, on_device(): pl.pallas_call(functools.partial(kernel, counts), out_shape=(jax.ShapeDty...  14.7 us
    pallas_call x1, Pallas kernels, on_device(): pl.pallas_call(write_out, out_shape=(jax.ShapeDtypeStruct(velocity.shape,...  0.83 us

profile of v4, /device:TPU:0, one launch (start us, length us, event | category | flops | bytes accessed | tf_op | source)
XLA Modules:
  0.0 16.2 jit_solution(5194786420456215607)
XLA Ops:
  0.6 14.7 %shard_map.59 = (f32[3,8,16,128]{3,2,1,0:T(8,128)S(1)}, f32[3,16,16,32]{3,2,1,0:T(8,128)S(1)}) custom-call(f32[3,8,16,128]{3,2,1,0:T(8,128)} %v_hbm.1, f32[3,8,16,128]{3,2,1,0:T(8,128)} %f_hbm.1, f32[8,16,128]{2,1,0:T(8,128)} %r_hbm.1, f32[128,128]{1,0:T(8,128)} %constant.2.clone.m_hbm), custom_call_target="tpu_custom_call" | custom-call | tf_op jit(solution)/shard_map/pallas_call | solution.py:669
  15.4 0.8 %shard_map.60 = (f32[3,8,16,128]{3,2,1,0:T(8,128)}, f32[3,16,16,32]{3,2,1,0:T(8,128)}) custom-call(f32[3,8,16,128]{3,2,1,0:T(8,128)S(1)} %get-tuple-element.6.vel_ref, f32[3,16,16,32]{3,2,1,0:T(8,128)S(1)} %get-tuple-element.7.comp_ref), custom_call_target="tpu_custom_call" | custom-call | tf_op jit(solution)/shard_map/pallas_call | solution.py:712

commit v5 on v4

--- a/solution.py
+++ b/solution.py
@@ -286,6 +286,7 @@
         (lambda x, t: f_at(0, x, t), lambda x, t: f_at(1, x, t)),
         (lambda x, t: f_at(2, x, t), lambda x, t: r_ext[2 + x, tile_of(t)]),
     )
+    from_ends = jnp.where(place < 4, 3 - place, Z + 3 - place)
     for t in near:
         turned = []
         for pair in held:
@@ -294,11 +295,8 @@
                 if get is not None:
                     for x in range(X):
                         at = (x + 4 + 8 * half) % 16
-                        packed = jnp.where(group == at, lane_roll(get(x, t), 8 * at + 3), packed)
-            out = jnp.where(place == 3, packed, lane_roll(packed, 6))
-            for spot, shift in ((2, -2), (1, -4), (4, 2), (5, 4)):
-                out = jnp.where(place == spot, lane_roll(packed, shift), out)
-            turned.append(out)
+                        packed = jnp.where(group == at, jnp.take_along_axis(get(x, t), from_ends, axis=1), packed)
+            turned.append(packed)
         for i in range(4):
             z_send[i, tile_of(t)] = turned[i]
             for side in range(2):
@@ -347,7 +345,9 @@
                             y * coefs : (y + 1) * coefs, place * chunk : (place + 1) * chunk
                         ]
 
-    lane_swap = lambda t: jnp.where(even_l, lane_roll(t, -1), lane_roll(t, 1))
+    lane_take = lambda t, source: jnp.take_along_axis(t, source, axis=1)
+    pair_of = lane + 1 - 2 * (lane % 2)
+    lane_swap = lambda t: lane_take(t, pair_of)
     row_swap = lambda t: jnp.where(even_r, row_roll(t, -1), row_roll(t, 1))
     slot_at = lane % 16
     corner_of = ((0, 0), (0, 1), (1, 1), (1, 0))
@@ -362,14 +362,12 @@
             out.append(jnp.where(even_l, left, right) + lane_swap(jnp.where(even_l, right, left)))
         return out
 
+    from_far = jnp.where(slot_at < 8, 6, Z + 6) - slot_at + 2 * (slot_at % 2)
+
     def edge_lanes(fields, t):
         packed = jnp.zeros((8, Z), f32)
         for start, field in fields:
-            for depth in range(1, 5):
-                high = (lane >= start + 8 - 2 * depth) & (lane < start + 10 - 2 * depth)
-                packed = jnp.where(high, lane_roll(field[t], start + 10 - 4 * depth), packed)
-                low = (lane >= start + 6 + 2 * depth) & (lane < start + 8 + 2 * depth)
-                packed = jnp.where(low, lane_roll(field[t], start + 6 + 4 * depth), packed)
+            packed = jnp.where((lane >= start) & (lane < start + 16), lane_take(field[t], from_far), packed)
         return packed
 
     coarse_weight = [
@@ -403,6 +401,20 @@
                     if spot:
                         moved = jnp.where(inside, moved, c_send[j, tile, k])
                     c_send[j, tile, k] = moved
+
+    for c in range(C):
+        for x in range(X):
+            for t in near:
+                own = v_at(c, x, t)
+                total = f_at(c, x, t) + jnp.where(lane == 0, 0.0, lane_roll(own, 1))
+                total = total + jnp.where(lane == Z - 1, 0.0, lane_roll(own, -1))
+                for other in range(max(x - 1, 0), min(x + 2, X)):
+                    if other != x:
+                        total = total + v_at(c, other, t)
+                for other, shift, inner in ((t + 1, -1, row < 7), (t - 1, 1, row >= 1)):
+                    beyond = row_roll(v_at(c, x, other), shift) if other in near else 0.0
+                    total = total + jnp.where(inner, row_roll(own, shift), beyond)
+                u1_ext[c, 2 + x, tile_of(t)] = keep * own + w_ext[2 + x, tile_of(t)] * total
 
     settle(fine_copies(), a_recv_sem.at[0])
 
@@ -476,8 +488,21 @@
         below = jnp.where(row >= by, row_roll(own, by), row_roll(get(before), by))
         return below, above
 
+    def rows_beside(at, t):
+        get = lambda t: at(tile_of(t))
+        if t < tiles_y:
+            above = at(pl.ds(t * 8 + 1, 8))
+        else:
+            above = jnp.where(row < 7, row_roll(get(t), -1), row_roll(get(0), -1))
+        if t > 0:
+            below = at(pl.ds(t * 8 - 1, 8))
+        else:
+            below = jnp.where(row >= 1, row_roll(get(t), 1), row_roll(get(tiles_y), 1))
+        return below, above
+
     def main_total(get, edge, c, x, t):
-        below, above = around_rows(lambda t: get(c, x, t), t, tiles_y + 1, 1)
+        below, above = rows_beside(lambda rows: get(c, x, rows), t)
+        get = lambda c, x, t, get=get: get(c, x, tile_of(t))
         total = (get(c, x - 1, t) + get(c, x + 1, t)) + (below + above)
         beside_z = lane_roll(edge[c, t], -(8 * (x + 4) + 4))
         own = get(c, x, t)
@@ -496,6 +521,9 @@
 
     u1_at = lambda c, x, t: u1_ext[c, 2 + x, tile_of(t)]
     u2_at = lambda c, x, t: u2_ext[c, 1 + x, tile_of(t)]
+    v_rows = lambda c, x, rows: v_ext[c, 3 + x, rows]
+    u1_rows = lambda c, x, rows: u1_ext[c, 2 + x, rows]
+    u2_rows = lambda c, x, rows: u2_ext[c, 1 + x, rows]
     w_at = lambda x, t: w_ext[2 + x, tile_of(t)]
 
     edge_1, edge_2 = {}, {}
@@ -504,8 +532,19 @@
             total = edge_total(v_at, edge_v, c, range(-1, X + 1), t)
             edge_1[c, t] = keep * edge_v[c, t] + edge_w[t] * (edge_f[c, t] + total)
         for x in range(-2, X + 2):
-            for t in near if x in (-2, X + 1) else ring:
-                total = main_total(v_at, edge_v, c, x, t)
+            if 0 <= x < X:
+                for t in near:
+                    beside_z = lane_roll(edge_v[c, t], -(8 * (x + 4) + 4))
+                    total = jnp.where((lane == 0) | (lane == Z - 1), beside_z, 0.0)
+                    if t == 0:
+                        total = total + jnp.where(row == 0, row_roll(v_at(c, x, tiles_y), 1), 0.0)
+                    if t == tiles_y - 1:
+                        total = total + jnp.where(row == 7, row_roll(v_at(c, x, tiles_y), -1), 0.0)
+                    if x in (0, X - 1):
+                        total = total + v_at(c, -1 if x == 0 else X, t)
+                    u1_ext[c, 2 + x, tile_of(t)] = u1_at(c, x, t) + w_at(x, t) * total
+            for t in near if x in (-2, X + 1) else [tiles_y] if 0 <= x < X else ring:
+                total = main_total(v_rows, edge_v, c, x, t)
                 u1_ext[c, 2 + x, tile_of(t)] = keep * v_at(c, x, t) + w_at(x, t) * (f_at(c, x, t) + total)
     for c in range(C):
         for t in near:
@@ -513,10 +552,10 @@
             edge_2[c, t] = keep * edge_1[c, t] + edge_w[t] * (edge_f[c, t] + total)
         for x in range(-1, X + 1):
             for t in near if x in (-1, X) else ring:
-                total = main_total(u1_at, edge_1, c, x, t)
+                total = main_total(u1_rows, edge_1, c, x, t)
                 u2_ext[c, 1 + x, tile_of(t)] = keep * u1_at(c, x, t) + w_at(x, t) * (f_at(c, x, t) + total)
     sums = [
-        [[main_total(u2_at, edge_2, c, x, t) + f_at(c, x, t) for t in near] for x in range(X)] for c in range(C)
+        [[main_total(u2_rows, edge_2, c, x, t) + f_at(c, x, t) for t in near] for x in range(X)] for c in range(C)
     ]
 
     correction = []

time: 16.3 us -> 16.1 us (0.988)
  Pallas kernels: 15.5 us -> 15.3 us
    pallas_call x1, Pallas kernels: 14.7 us -> 14.4 us  [on_device(): pl.pallas_call(functools.partial(kernel, counts), out_shape=(jax.ShapeDty...]
where the time goes in v5:
time: 16.1 us; the launch traced here: 15.9 us
  Pallas kernels  15.3 us (95%)
  between operations  0.64 us (4%)
    pallas_call x1, Pallas kernels, on_device(): pl.pallas_call(functools.partial(kernel, counts), out_shape=(jax.ShapeDty...  14.4 us
    pallas_call x1, Pallas kernels, on_device(): pl.pallas_call(write_out, out_shape=(jax.ShapeDtypeStruct(velocity.shape,...  0.83 us

profile of v5, /device:TPU:0, one launch (start us, length us, event | category | flops | bytes accessed | tf_op | source)
XLA Modules:
  0.0 15.9 jit_solution(8880004578263395355)
XLA Ops:
  0.6 14.4 %shard_map.59 = (f32[3,8,16,128]{3,2,1,0:T(8,128)S(1)}, f32[3,16,16,32]{3,2,1,0:T(8,128)S(1)}) custom-call(f32[3,8,16,128]{3,2,1,0:T(8,128)} %v_hbm.1, f32[3,8,16,128]{3,2,1,0:T(8,128)} %f_hbm.1, f32[8,16,128]{2,1,0:T(8,128)} %r_hbm.1, f32[128,128]{1,0:T(8,128)} %constant.2.clone.m_hbm), custom_call_target="tpu_custom_call" | custom-call | tf_op jit(solution)/shard_map/pallas_call | solution.py:708
  15.1 0.8 %shard_map.60 = (f32[3,8,16,128]{3,2,1,0:T(8,128)}, f32[3,16,16,32]{3,2,1,0:T(8,128)}) custom-call(f32[3,8,16,128]{3,2,1,0:T(8,128)S(1)} %get-tuple-element.6.vel_ref, f32[3,16,16,32]{3,2,1,0:T(8,128)S(1)} %get-tuple-element.7.comp_ref), custom_call_target="tpu_custom_call" | custom-call | tf_op jit(solution)/shard_map/pallas_call | solution.py:751

commit v6 on v5

--- a/solution.py
+++ b/solution.py
@@ -62,7 +62,7 @@
 def kernel(
     sizes, v_hbm, f_hbm, r_hbm, m_hbm, vel_ref, comp_ref, v_ext, f_ext, r_ext, m_ref, w_ext, u1_ext, u2_ext,
     y_send, y_recv, xy_send, xy_recv, z_send, z_recv, yz_send, yz_recv, xz_send, xz_recv, corner_recv,
-    q_ext, h_ext, zs_coarse, c_send, c_recv, measure,
+    q_ext, h_ext, zs_coarse, c_send, c_recv, measure, band_ref, pairs_ref,
     a_send_sem, a_recv_sem, q_send_sem, q_recv_sem, c_send_sem, c_recv_sem, in_sem,
 ):
     counts = sizes
@@ -383,6 +383,28 @@
         for t in near:
             w_ext[2 + x, tile_of(t)] = damping / (6.0 + r_ext[2 + x, tile_of(t)])
 
+    source = lax.broadcasted_iota(jnp.int32, (Z, Z), 0)
+    target = lax.broadcasted_iota(jnp.int32, (Z, Z), 1)
+    apart = jnp.abs(source - target)
+    band = jnp.where(apart == 1, 1.0, 0.0).astype(jnp.bfloat16)
+    paired = (apart == 2) | ((apart == 1) & (source // 2 == target // 2))
+    pairs = jnp.where(paired, 1.0, 0.0).astype(jnp.bfloat16)
+    for part in range(3):
+        band_ref[part * Z : part * Z + Z] = band
+        pairs_ref[part * Z : part * Z + Z] = pairs
+
+    def lane_sums(tiles, matrix):
+        stack = jnp.concatenate(tiles, axis=0)
+        high = stack.astype(jnp.bfloat16)
+        rest = stack - high.astype(f32)
+        middle = rest.astype(jnp.bfloat16)
+        low = (rest - middle.astype(f32)).astype(jnp.bfloat16)
+        done = lax.dot_general(
+            jnp.concatenate([high, middle, low], axis=1), matrix[...], (((1,), (0,)), ((), ())),
+            preferred_element_type=f32,
+        )
+        return [done[i * 8 : i * 8 + 8] for i in range(len(tiles))]
+
     levels = local_levels(X)
     for c in range(C):
         for t in near:
@@ -500,11 +522,13 @@
             below = jnp.where(row >= 1, row_roll(get(t), 1), row_roll(get(tiles_y), 1))
         return below, above
 
-    def main_total(get, edge, c, x, t):
+    def main_total(get, edge, c, x, t, along_z=None):
         below, above = rows_beside(lambda rows: get(c, x, rows), t)
         get = lambda c, x, t, get=get: get(c, x, tile_of(t))
         total = (get(c, x - 1, t) + get(c, x + 1, t)) + (below + above)
         beside_z = lane_roll(edge[c, t], -(8 * (x + 4) + 4))
+        if along_z is not None:
+            return total + (along_z + jnp.where((lane == 0) | (lane == Z - 1), beside_z, 0.0))
         own = get(c, x, t)
         total = total + jnp.where(lane == 0, beside_z, lane_roll(own, 1))
         return total + jnp.where(lane == Z - 1, beside_z, lane_roll(own, -1))
@@ -531,6 +555,12 @@
         for t in ring:
             total = edge_total(v_at, edge_v, c, range(-1, X + 1), t)
             edge_1[c, t] = keep * edge_v[c, t] + edge_w[t] * (edge_f[c, t] + total)
+        chosen = [
+            (x, t)
+            for x in range(-2, X + 2)
+            for t in (near if x in (-2, X + 1) else [tiles_y] if 0 <= x < X else ring)
+        ]
+        along_z = dict(zip(chosen, lane_sums([v_at(c, x, t) for x, t in chosen], band_ref)))
         for x in range(-2, X + 2):
             if 0 <= x < X:
                 for t in near:
@@ -544,19 +574,25 @@
                         total = total + v_at(c, -1 if x == 0 else X, t)
                     u1_ext[c, 2 + x, tile_of(t)] = u1_at(c, x, t) + w_at(x, t) * total
             for t in near if x in (-2, X + 1) else [tiles_y] if 0 <= x < X else ring:
-                total = main_total(v_rows, edge_v, c, x, t)
+                total = main_total(v_rows, edge_v, c, x, t, along_z[x, t])
                 u1_ext[c, 2 + x, tile_of(t)] = keep * v_at(c, x, t) + w_at(x, t) * (f_at(c, x, t) + total)
     for c in range(C):
         for t in near:
             total = edge_total(u1_at, edge_1, c, range(X), t)
             edge_2[c, t] = keep * edge_1[c, t] + edge_w[t] * (edge_f[c, t] + total)
+        chosen = [(x, t) for x in range(-1, X + 1) for t in (near if x in (-1, X) else ring)]
+        along_z = dict(zip(chosen, lane_sums([u1_at(c, x, t) for x, t in chosen], band_ref)))
         for x in range(-1, X + 1):
             for t in near if x in (-1, X) else ring:
-                total = main_total(u1_rows, edge_1, c, x, t)
+                total = main_total(u1_rows, edge_1, c, x, t, along_z[x, t])
                 u2_ext[c, 1 + x, tile_of(t)] = keep * u1_at(c, x, t) + w_at(x, t) * (f_at(c, x, t) + total)
-    sums = [
-        [[main_total(u2_rows, edge_2, c, x, t) + f_at(c, x, t) for t in near] for x in range(X)] for c in range(C)
-    ]
+    sums = []
+    for c in range(C):
+        chosen = [(x, t) for x in range(X) for t in near]
+        along_z = dict(zip(chosen, lane_sums([u2_at(c, x, t) for x, t in chosen], band_ref)))
+        sums.append([
+            [main_total(u2_rows, edge_2, c, x, t, along_z[x, t]) + f_at(c, x, t) for t in near] for x in range(X)
+        ])
 
     correction = []
     for c in range(C):
@@ -606,7 +642,7 @@
     def along(get, b, t):
         low, high = get(max(b - 1, 0), t), get(min(b + 1, 2), t)
         across = jnp.where(even_l, jnp.where(even_r, high, low), get(b, t))
-        return lane_swap(get(b, t)) + row_swap(across)
+        return row_swap(across)
 
     def inject(edge, b, c, t):
         return lane_roll(edge[b, t], -(16 * c + 8))
@@ -619,12 +655,14 @@
 
     def coarse_sweep(main, edge, main_at, edge_at):
         new_main, new_edge = dict(main), dict(edge)
-        for b, t in main_at:
-            for c in range(C):
+        for c in range(C):
+            lanes = dict(zip(main_at, lane_sums([main[b, c, t] for b, t in main_at], pairs_ref)))
+            for b, t in main_at:
                 get = lambda b, t, c=c: main[b, c, t]
                 row_get = lambda t, b=b, c=c: main[b, c, t]
                 total = along(get, b, t) + (above(row_get, t) + below(row_get, t))
-                total = total + (left_of(main, edge, b, c, t) + right_of(main, edge, b, c, t))
+                ends = jnp.where((lane < 2) | (lane >= Z - 2), inject(edge, b, c, t), 0.0)
+                total = total + (lanes[b, t] + ends)
                 new_main[b, c, t] = keep * main[b, c, t] + first_main[b, c, t] + step_main[b, t] * total
         for b, t in edge_at:
             get = lambda b, t: edge[b, t]
@@ -632,7 +670,7 @@
             own = lane_roll(main[b, 0, t], 8)
             for c in range(1, C):
                 own = jnp.where(lane < 16 * c, own, lane_roll(main[b, c, t], 16 * c + 8))
-            total = along(get, b, t) + (above(row_get, t) + below(row_get, t))
+            total = along(get, b, t) + lane_swap(edge[b, t]) + (above(row_get, t) + below(row_get, t))
             total = total + jnp.where((slot_at == 8) | (slot_at == 9), own, lane_roll(edge[b, t], 2))
             total = total + jnp.where((slot_at == 6) | (slot_at == 7), own, lane_roll(edge[b, t], -2))
             new_edge[b, t] = keep * edge[b, t] + first_edge[b, t] + step_edge[b, t] * total
@@ -738,6 +776,8 @@
             space(blocks, tiles, kept, 8, Z),
             space(blocks, tiles, kept, 8, Z),
             space(max((blocks - 1) * tiles * kept * 8, 128 * Y), Z),
+            pltpu.VMEM((3 * Z, Z), jnp.bfloat16),
+            pltpu.VMEM((3 * Z, Z), jnp.bfloat16),
             pltpu.SemaphoreType.DMA((1,)),
             pltpu.SemaphoreType.DMA((1,)),
             pltpu.SemaphoreType.DMA((2,)),

time: 16.1 us -> 15.8 us (0.981)
  Pallas kernels: 15.3 us -> 15 us
    pallas_call x1, Pallas kernels: 14.4 us -> 14.2 us  [on_device(): pl.pallas_call(functools.partial(kernel, counts), out_shape=(jax.ShapeDty...]
where the time goes in v6:
time: 15.8 us; the launch traced here: 15.7 us
  Pallas kernels  15 us (95%)
  between operations  0.64 us (4%)
    pallas_call x1, Pallas kernels, on_device(): pl.pallas_call(functools.partial(kernel, counts), out_shape=(jax.ShapeDty...  14.2 us
    pallas_call x1, Pallas kernels, on_device(): pl.pallas_call(write_out, out_shape=(jax.ShapeDtypeStruct(velocity.shape,...  0.83 us

profile of v6, /device:TPU:0, one launch (start us, length us, event | category | flops | bytes accessed | tf_op | source)
XLA Modules:
  0.0 15.7 jit_solution(6029458477324613876)
XLA Ops:
  0.6 14.2 %shard_map.59 = (f32[3,8,16,128]{3,2,1,0:T(8,128)S(1)}, f32[3,16,16,32]{3,2,1,0:T(8,128)S(1)}) custom-call(f32[3,8,16,128]{3,2,1,0:T(8,128)} %v_hbm.1, f32[3,8,16,128]{3,2,1,0:T(8,128)} %f_hbm.1, f32[8,16,128]{2,1,0:T(8,128)} %r_hbm.1, f32[128,128]{1,0:T(8,128)} %constant.2.clone.m_hbm), custom_call_target="tpu_custom_call" | custom-call | tf_op jit(solution)/shard_map/pallas_call | solution.py:746
  14.9 0.8 %shard_map.60 = (f32[3,8,16,128]{3,2,1,0:T(8,128)}, f32[3,16,16,32]{3,2,1,0:T(8,128)}) custom-call(f32[3,8,16,128]{3,2,1,0:T(8,128)S(1)} %get-tuple-element.6.vel_ref, f32[3,16,16,32]{3,2,1,0:T(8,128)S(1)} %get-tuple-element.7.comp_ref), custom_call_target="tpu_custom_call" | custom-call | tf_op jit(solution)/shard_map/pallas_call | solution.py:791

commit v7 on v6

--- a/solution.py
+++ b/solution.py
@@ -56,17 +56,31 @@
     return sorted(found, key=lambda sides: (-len(sides), sides))
 
 
+def lane_sums(tiles, matrix):
+    stack = jnp.concatenate(tiles, axis=0)
+    high = stack.astype(jnp.bfloat16)
+    rest = stack - high.astype(jnp.float32)
+    middle = rest.astype(jnp.bfloat16)
+    low = (rest - middle.astype(jnp.float32)).astype(jnp.bfloat16)
+    done = lax.dot_general(
+        jnp.concatenate([high, middle, low], axis=1), matrix[...], (((1,), (0,)), ((), ())),
+        preferred_element_type=jnp.float32,
+    )
+    return [done[i * 8 : i * 8 + 8] for i in range(len(tiles))]
+
+
 far = 1e30
 
 
 def kernel(
-    sizes, v_hbm, f_hbm, r_hbm, m_hbm, vel_ref, comp_ref, v_ext, f_ext, r_ext, m_ref, w_ext, u1_ext, u2_ext,
+    sizes, v_hbm, f_hbm, r_hbm, m_hbm, comp_ref, base_ref, w_ext, q_ext, h_ext, pairs_ref,
+    v_ext, f_ext, r_ext, m_ref, u1_ext, u2_ext,
     y_send, y_recv, xy_send, xy_recv, z_send, z_recv, yz_send, yz_recv, xz_send, xz_recv, corner_recv,
-    q_ext, h_ext, zs_coarse, c_send, c_recv, measure, band_ref, pairs_ref,
+    zs_coarse, c_send, c_recv, measure, band_ref,
     a_send_sem, a_recv_sem, q_send_sem, q_recv_sem, c_send_sem, c_recv_sem, in_sem,
 ):
     counts = sizes
-    C, X, Y, Z = vel_ref.shape
+    C, X, Y, Z = base_ref.shape
     me = {axis: lax.axis_index(axis) for axis in counts}
     blocks = counts["gx"]
     chunk = Z // blocks
@@ -119,7 +133,6 @@
     place = lane % 8
     group = lane // 8
     low_half = (lane < 32) | (lane >= 96)
-    near_groups = (group % 8 == 2) | (group % 8 == 3) | (group % 8 == 4) | (group % 8 == 5)
 
     def fine_messages(sides):
         at = {axis: high for axis, high in sides}
@@ -245,6 +258,7 @@
     even_r = row % 2 == 0
     lane_roll = lambda t, shift: pltpu.roll(t, shift % Z, 1) if shift % Z else t
     row_roll = lambda t, shift: pltpu.roll(t, shift % 8, 0)
+    lane_take = lambda t, source: jnp.take_along_axis(t, source, axis=1)
     v_flat = v_ext.reshape(C * (X + 6) * rows_ext, Z)
     f_flat = f_ext.reshape(C * (X + 4) * rows_ext, Z)
     r_flat = r_ext.reshape((X + 4) * rows_ext, Z)
@@ -288,15 +302,19 @@
     )
     from_ends = jnp.where(place < 4, 3 - place, Z + 3 - place)
     for t in near:
-        turned = []
-        for pair in held:
+        turned, crossed = [], []
+        for i, pair in enumerate(held):
             packed = jnp.zeros((8, Z), f32)
+            across = jnp.zeros((8, Z), f32) if i % 2 == 0 else crossed.pop()
             for half, get in enumerate(pair):
                 if get is not None:
                     for x in range(X):
-                        at = (x + 4 + 8 * half) % 16
-                        packed = jnp.where(group == at, jnp.take_along_axis(get(x, t), from_ends, axis=1), packed)
+                        ends = lane_take(get(x, t), from_ends)
+                        packed = jnp.where(group == (x + 4 + 8 * half) % 16, ends, packed)
+                        if x < 2 or x >= X - 2:
+                            across = jnp.where(group == (x + 4 + 8 * half + 4 * (i % 2)) % 16, ends, across)
             turned.append(packed)
+            crossed.append(across)
         for i in range(4):
             z_send[i, tile_of(t)] = turned[i]
             for side in range(2):
@@ -304,7 +322,7 @@
                     first = 6 if side else 0
                     yz_send[side, 2 * i : 2 * i + 2] = turned[i][first : first + 2]
         for i in range(2):
-            xz_send[i, tile_of(t)] = jnp.where(near_groups, turned[2 * i], lane_roll(turned[2 * i + 1], 32))
+            xz_send[i, tile_of(t)] = crossed[i]
     pl.semaphore_wait(barrier, expected)
     for sides, copy in fine_copies():
         pl.when(all_exist(sides, False))(copy.start)
@@ -345,24 +363,28 @@
                             y * coefs : (y + 1) * coefs, place * chunk : (place + 1) * chunk
                         ]
 
-    lane_take = lambda t, source: jnp.take_along_axis(t, source, axis=1)
     pair_of = lane + 1 - 2 * (lane % 2)
     lane_swap = lambda t: lane_take(t, pair_of)
     row_swap = lambda t: jnp.where(even_r, row_roll(t, -1), row_roll(t, 1))
     slot_at = lane % 16
     corner_of = ((0, 0), (0, 1), (1, 1), (1, 0))
 
-    def pooled(planes):
+    def pooled_halves(planes):
         pairs = [[planes[x][t] + planes[x + 1][t] for t in near] for x in range(0, X, 2)]
         out = []
         for t in near:
             t0, t1, t2, t3 = (pair[t] for pair in pairs)
             left = jnp.where(even_r, t0, t3) + row_swap(jnp.where(even_r, t3, t0))
             right = jnp.where(even_r, t1, t2) + row_swap(jnp.where(even_r, t2, t1))
-            out.append(jnp.where(even_l, left, right) + lane_swap(jnp.where(even_l, right, left)))
+            out.append((jnp.where(even_l, left, right), jnp.where(even_l, right, left)))
         return out
 
+    def pooled(planes):
+        return [own + lane_swap(other) for own, other in pooled_halves(planes)]
+
     from_far = jnp.where(slot_at < 8, 6, Z + 6) - slot_at + 2 * (slot_at % 2)
+
+    from_far_pair = from_far + 1 - 2 * (from_far % 2)
 
     def edge_lanes(fields, t):
         packed = jnp.zeros((8, Z), f32)
@@ -376,9 +398,9 @@
     ]
     coarse_step = [0.25 * weight for weight in coarse_weight]
     step_edges = [edge_lanes([(64 + 16 * c, coarse_step) for c in range(C)], t) for t in near]
+    weight_edges = [edge_lanes([(16 * c, coarse_weight) for c in range(C)], t) for t in near]
     for t in near:
         q_ext[1, C, tile_of(t)] = coarse_step[t]
-        zs_coarse[tile_of(t)] = step_edges[t]
     for x in range(X):
         for t in near:
             w_ext[2 + x, tile_of(t)] = damping / (6.0 + r_ext[2 + x, tile_of(t)])
@@ -392,18 +414,6 @@
     for part in range(3):
         band_ref[part * Z : part * Z + Z] = band
         pairs_ref[part * Z : part * Z + Z] = pairs
-
-    def lane_sums(tiles, matrix):
-        stack = jnp.concatenate(tiles, axis=0)
-        high = stack.astype(jnp.bfloat16)
-        rest = stack - high.astype(f32)
-        middle = rest.astype(jnp.bfloat16)
-        low = (rest - middle.astype(f32)).astype(jnp.bfloat16)
-        done = lax.dot_general(
-            jnp.concatenate([high, middle, low], axis=1), matrix[...], (((1,), (0,)), ((), ())),
-            preferred_element_type=f32,
-        )
-        return [done[i * 8 : i * 8 + 8] for i in range(len(tiles))]
 
     levels = local_levels(X)
     for c in range(C):
@@ -594,20 +604,29 @@
             [main_total(u2_rows, edge_2, c, x, t, along_z[x, t]) + f_at(c, x, t) for t in near] for x in range(X)
         ])
 
-    correction = []
-    for c in range(C):
-        rhs = pooled([
+    halves = [
+        pooled_halves([
             [sums[c][x][t] - (6.0 + r_ext[2 + x, tile_of(t)]) * u2_at(c, x, t) for t in near] for x in range(X)
         ])
-        correction.append([weight * (0.125 * total) for weight, total in zip(coarse_weight, rhs)])
-    for c in range(C):
-        for t in near:
-            q_ext[1, c, tile_of(t)] = correction[c][t]
+        for c in range(C)
+    ]
     for t in near:
-        edges_t = edge_lanes([(16 * c, correction[c]) for c in range(C)], t)
-        zs_coarse[tile_of(t)] = jnp.where(lane < 64, edges_t, zs_coarse[tile_of(t)])
+        total = jnp.zeros((8, Z), f32)
+        for c in range(C):
+            own, other = halves[c][t]
+            here = (lane >= 16 * c) & (lane < 16 * c + 16)
+            total = jnp.where(here, lane_take(own, from_far) + lane_take(other, from_far_pair), total)
+        zs_coarse[tile_of(t)] = jnp.where(lane < 64, weight_edges[t] * (0.125 * total), step_edges[t])
+        for c in range(C):
+            own, other = halves[c][t]
+            q_ext[1, c, tile_of(t)] = coarse_weight[t] * (0.125 * (own + lane_swap(other)))
     for sides, copy in coarse_copies():
         pl.when(all_exist(sides, False))(copy.start)
+
+    for c in range(C):
+        for x in range(X):
+            for t in near:
+                base_ref[c, x, tile_of(t)] = keep * u2_at(c, x, t) + w_at(x, t) * sums[c][x][t]
 
     for j in range(blocks):
         @pl.when(me["gx"] == j)
@@ -620,6 +639,32 @@
 
     settle(step_copies(), q_recv_sem.at[1])
     settle(coarse_copies(), q_recv_sem.at[0])
+
+    settle(fine_copies(), a_send_sem.at[0])
+    settle(step_copies(), q_send_sem.at[1])
+    settle(coarse_copies(), q_send_sem.at[0])
+    settle_parts(c_send_sem.at[0])
+
+
+def finish(base_ref, w_ext, q_ext, h_ext, pairs_ref, comp_ref, vel_hbm, comp_hbm, vel_ref, sem):
+    C, X, Y, Z = base_ref.shape
+    f32 = jnp.float32
+    comp_copy = pltpu.make_async_copy(comp_ref, comp_hbm, sem.at[C])
+    comp_copy.start()
+    tiles_y = Y // 8
+    near = range(tiles_y)
+    tile_of = lambda t: slice(t * 8, t * 8 + 8)
+    lane = lax.broadcasted_iota(jnp.int32, (8, Z), 1)
+    row = lax.broadcasted_iota(jnp.int32, (8, Z), 0)
+    even_l = lane % 2 == 0
+    even_r = row % 2 == 0
+    slot_at = lane % 16
+    corner_of = ((0, 0), (0, 1), (1, 1), (1, 0))
+    pair_of = lane + 1 - 2 * (lane % 2)
+    lane_roll = lambda t, shift: pltpu.roll(t, shift % Z, 1) if shift % Z else t
+    row_roll = lambda t, shift: pltpu.roll(t, shift % 8, 0)
+    lane_swap = lambda t: jnp.take_along_axis(t, pair_of, axis=1)
+    row_swap = lambda t: jnp.where(even_r, row_roll(t, -1), row_roll(t, 1))
 
     ring = range(tiles_y + 2)
     after = lambda t: (t + 1) % len(ring)
@@ -693,6 +738,7 @@
             return jnp.where(even_l, even, lane_roll(odd, 1))
         return jnp.where(even_l, lane_roll(even, -1), odd)
 
+    copies = []
     for c in range(C):
         for t in near:
             at = tile_of(t)
@@ -713,23 +759,10 @@
                 p = x // 2
                 pa, pb = corner_of[p]
                 added = spread_rows(wide[0][pb], wide[1][pb], pa) + spread[p + 2 * (x % 2)]
-                total = sums[c][x][t] + added
-                vel_ref[c, x, at] = keep * (u2_at(c, x, t) + spread[p + 1]) + w_at(x, t) * total
-
-    settle(fine_copies(), a_send_sem.at[0])
-    settle(step_copies(), q_send_sem.at[1])
-    settle(coarse_copies(), q_send_sem.at[0])
-    settle_parts(c_send_sem.at[0])
-
-
-def write_out(vel_ref, comp_ref, vel_hbm, comp_hbm, sem):
-    copies = [
-        pltpu.make_async_copy(comp_ref, comp_hbm, sem.at[0]),
-        pltpu.make_async_copy(vel_ref, vel_hbm, sem.at[1]),
-    ]
-    for copy in copies:
-        copy.start()
-    for copy in copies:
+                vel_ref[c, x, at] = base_ref[c, x, at] + keep * spread[p + 1] + w_ext[2 + x, at] * added
+        copies.append(pltpu.make_async_copy(vel_ref.at[c], vel_hbm.at[c], sem.at[c]))
+        copies[-1].start()
+    for copy in [comp_copy] + copies:
         copy.wait()
 
 
@@ -743,20 +776,23 @@
     vmem = pl.BlockSpec(memory_space=pltpu.VMEM)
     space = lambda *shape: pltpu.VMEM(shape, jnp.float32)
 
-    velocity, compressed = pl.pallas_call(
+    compressed, *kept_arrays = pl.pallas_call(
         functools.partial(kernel, counts),
-        out_shape=(
+        out_shape=[
+            jax.ShapeDtypeStruct((C, Y, kept * blocks, chunk), jnp.float32),
             jax.ShapeDtypeStruct((C, X, Y, Z), jnp.float32),
-            jax.ShapeDtypeStruct((C, Y, kept * blocks, chunk), jnp.float32),
-        ),
+            jax.ShapeDtypeStruct((X + 4, Y + 8, Z), jnp.float32),
+            jax.ShapeDtypeStruct((3, C + 1, Y + 16, Z), jnp.float32),
+            jax.ShapeDtypeStruct((2, 3, Y + 16, Z), jnp.float32),
+            jax.ShapeDtypeStruct((3 * Z, Z), jnp.bfloat16),
+        ],
         in_specs=[pl.BlockSpec(memory_space=pltpu.HBM)] * 4,
-        out_specs=(vmem, vmem),
+        out_specs=[vmem] * 6,
         scratch_shapes=[
             space(C, X + 6, Y + 8, Z),
             space(C, X + 4, Y + 8, Z),
             space(X + 4, Y + 8, Z),
             space(*matrix.shape),
-            space(X + 4, Y + 8, Z),
             space(C, X + 4, Y + 8, Z),
             space(C, X + 2, Y + 8, Z),
             space(2, 5 * C + 2, X, Z),
@@ -770,13 +806,10 @@
             space(2, Y, Z),
             space(2, 2, 2, Y, Z),
             space(2, 2, 2, 8, Z),
-            space(3, C + 1, Y + 16, Z),
-            space(2, 3, Y + 16, Z),
             space(Y, Z),
             space(blocks, tiles, kept, 8, Z),
             space(blocks, tiles, kept, 8, Z),
             space(max((blocks - 1) * tiles * kept * 8, 128 * Y), Z),
-            pltpu.VMEM((3 * Z, Z), jnp.bfloat16),
             pltpu.VMEM((3 * Z, Z), jnp.bfloat16),
             pltpu.SemaphoreType.DMA((1,)),
             pltpu.SemaphoreType.DMA((1,)),
@@ -789,16 +822,16 @@
         compiler_params=pltpu.CompilerParams(collective_id=0, has_side_effects=True, vmem_limit_bytes=40000000),
     )(*(pltpu.with_memory_space_constraint(a, pltpu.HBM) for a in (velocity_prev, forcing, reaction, matrix)))
     velocity, compressed = pl.pallas_call(
-        write_out,
+        finish,
         out_shape=(
-            jax.ShapeDtypeStruct(velocity.shape, jnp.float32),
+            jax.ShapeDtypeStruct((C, X, Y, Z), jnp.float32),
             jax.ShapeDtypeStruct(compressed.shape, jnp.float32),
         ),
-        in_specs=[vmem, vmem],
+        in_specs=[vmem] * 6,
         out_specs=[pl.BlockSpec(memory_space=pltpu.HBM)] * 2,
-        scratch_shapes=[pltpu.SemaphoreType.DMA((2,))],
-        compiler_params=pltpu.CompilerParams(vmem_limit_bytes=4000000),
-    )(velocity, compressed)
+        scratch_shapes=[space(C, X, Y, Z), pltpu.SemaphoreType.DMA((C + 1,))],
+        compiler_params=pltpu.CompilerParams(vmem_limit_bytes=16000000),
+    )(*kept_arrays, compressed)
     return velocity, jnp.swapaxes(compressed, 2, 3)
 
 

time: 15.8 us -> 15.7 us (level)
  no operation moved by 1% of the time
where the time goes in v7:
time: 15.7 us; the launch traced here: 15.5 us
  Pallas kernels  14.9 us (95%)
  between operations  0.64 us (4%)
    pallas_call x1, Pallas kernels, on_device(): pl.pallas_call(functools.partial(kernel, counts), out_shape=[jax.ShapeDty...  13.4 us
    pallas_call x1, Pallas kernels, on_device(): pl.pallas_call(finish, out_shape=(jax.ShapeDtypeStruct((C, X, Y, Z), jnp....  1.48 us

profile of v7, /device:TPU:0, one launch (start us, length us, event | category | flops | bytes accessed | tf_op | source)
XLA Modules:
  0.0 15.5 jit_solution(14921114481861342667)
XLA Ops:
  0.6 13.4 %shard_map.59 = (f32[3,16,16,32]{3,2,1,0:T(8,128)S(1)}, f32[3,8,16,128]{3,2,1,0:T(8,128)S(1)}, f32[12,24,128]{2,1,0:T(8,128)S(1)}, f32[3,4,32,128]{3,2,1,0:T(8,1...) custom-call(f32[3,8,16,128]{3,2,1,0:T(8,128)} %v_hbm.1, f32[3,8,16,128]{3,2,1,0:T(8,128)} %f_hbm.1, ...), custom_call_target="tpu_custom_call" | custom-call | tf_op jit(solution)/shard_map/pallas_call | solution.py:779
  14.1 1.5 %shard_map.60 = (f32[3,8,16,128]{3,2,1,0:T(8,128)}, f32[3,16,16,32]{3,2,1,0:T(8,128)}) custom-call(f32[3,8,16,128]{3,2,1,0:T(8,128)S(1)} %get-tuple-element.10.base_ref, f32[12,24,128]{2,1,0:T(8,128)S(1)} %get-tuple-element.11.w_ext, f32[3,4,32,128]{3,2,1,0:T(8,128)S(1)} %get-tuple-element.12.q_ext, f32[2,3,32,128]{3,2,1,0:T(8,128)S(1)} %get-tuple-element.13.h_ext, ...), custom_call_target="tpu_custom_call" | custom-call | tf_op jit(solution)/shard_map/pallas_call | solution.py:824

commit v8 on v7

--- a/solution.py
+++ b/solution.py
@@ -89,12 +89,11 @@
 
     loads = [
         pltpu.make_async_copy(src, dst, in_sem.at[i])
-        for i, (src, dst) in enumerate((
-            (v_hbm, v_ext.at[:, 3 : 3 + X, :Y]),
-            (f_hbm, f_ext.at[:, 2 : 2 + X, :Y]),
-            (r_hbm, r_ext.at[2 : 2 + X, :Y]),
-            (m_hbm, m_ref),
-        ))
+        for i, (src, dst) in enumerate(
+            [(v_hbm.at[c], v_ext.at[c, 3 : 3 + X, :Y]) for c in range(C)]
+            + [(f_hbm.at[c], f_ext.at[c, 2 : 2 + X, :Y]) for c in range(C)]
+            + [(r_hbm, r_ext.at[2 : 2 + X, :Y]), (m_hbm, m_ref)]
+        )
     ]
     for load in loads:
         load.start()
@@ -274,9 +273,38 @@
 
     depth_of = lambda number: number % 3 if number < 3 * C else (number - 3 * C) % 2
 
-    loads[0].wait()
-    loads[1].wait()
-    loads[2].wait()
+    v_at = lambda c, x, t: v_ext[c, 3 + x, tile_of(t)]
+    f_at = lambda c, x, t: f_ext[c, 2 + x, tile_of(t)]
+    held = (
+        (lambda x, t: v_at(0, x, t), lambda x, t: v_at(1, x, t)),
+        (lambda x, t: v_at(2, x, t), None),
+        (lambda x, t: f_at(0, x, t), lambda x, t: f_at(1, x, t)),
+        (lambda x, t: f_at(2, x, t), lambda x, t: r_ext[2 + x, tile_of(t)]),
+    )
+    from_ends = jnp.where(place < 4, 3 - place, Z + 3 - place)
+    needed = ((0, 1), (2,), (3, 4), (5, 6))
+    across = {}
+    for i, pair in enumerate(held):
+        for number in needed[i]:
+            loads[number].wait()
+        for t in near:
+            packed = jnp.zeros((8, Z), f32)
+            crossed = across.get(t, packed) if i % 2 else packed
+            for half, get in enumerate(pair):
+                if get is not None:
+                    for x in range(X):
+                        ends = lane_take(get(x, t), from_ends)
+                        packed = jnp.where(group == (x + 4 + 8 * half) % 16, ends, packed)
+                        if x < 2 or x >= X - 2:
+                            crossed = jnp.where(group == (x + 4 + 8 * half + 4 * (i % 2)) % 16, ends, crossed)
+            across[t] = crossed
+            z_send[i, tile_of(t)] = packed
+            if i % 2:
+                xz_send[i // 2, tile_of(t)] = crossed
+            for side in range(2):
+                if t == (tiles_y - 1 if side else 0):
+                    first = 6 if side else 0
+                    yz_send[side, 2 * i : 2 * i + 2] = packed[first : first + 2]
     for number in range(5 * C + 2):
         for side in range(2):
             depth = depth_of(number)
@@ -292,37 +320,6 @@
                     target[3 * c + i : 3 * c + i + 1] = v_ext[c, 3 + x, y : y + 1]
                 target[3 * C + c : 3 * C + c + 1] = f_ext[c, 2 + xs[0], ys[0] : ys[0] + 1]
             target[4 * C : 4 * C + 1] = r_ext[2 + xs[0], ys[0] : ys[0] + 1]
-    v_at = lambda c, x, t: v_ext[c, 3 + x, tile_of(t)]
-    f_at = lambda c, x, t: f_ext[c, 2 + x, tile_of(t)]
-    held = (
-        (lambda x, t: v_at(0, x, t), lambda x, t: v_at(1, x, t)),
-        (lambda x, t: v_at(2, x, t), None),
-        (lambda x, t: f_at(0, x, t), lambda x, t: f_at(1, x, t)),
-        (lambda x, t: f_at(2, x, t), lambda x, t: r_ext[2 + x, tile_of(t)]),
-    )
-    from_ends = jnp.where(place < 4, 3 - place, Z + 3 - place)
-    for t in near:
-        turned, crossed = [], []
-        for i, pair in enumerate(held):
-            packed = jnp.zeros((8, Z), f32)
-            across = jnp.zeros((8, Z), f32) if i % 2 == 0 else crossed.pop()
-            for half, get in enumerate(pair):
-                if get is not None:
-                    for x in range(X):
-                        ends = lane_take(get(x, t), from_ends)
-                        packed = jnp.where(group == (x + 4 + 8 * half) % 16, ends, packed)
-                        if x < 2 or x >= X - 2:
-                            across = jnp.where(group == (x + 4 + 8 * half + 4 * (i % 2)) % 16, ends, across)
-            turned.append(packed)
-            crossed.append(across)
-        for i in range(4):
-            z_send[i, tile_of(t)] = turned[i]
-            for side in range(2):
-                if t == (tiles_y - 1 if side else 0):
-                    first = 6 if side else 0
-                    yz_send[side, 2 * i : 2 * i + 2] = turned[i][first : first + 2]
-        for i in range(2):
-            xz_send[i, tile_of(t)] = crossed[i]
     pl.semaphore_wait(barrier, expected)
     for sides, copy in fine_copies():
         pl.when(all_exist(sides, False))(copy.start)
@@ -634,7 +631,7 @@
             c_recv[j] = c_send[j]
 
     settle_parts(c_recv_sem.at[0])
-    loads[3].wait()
+    loads[-1].wait()
     finish_compressed(range(c_send.shape[1]))
 
     settle(step_copies(), q_recv_sem.at[1])
@@ -817,7 +814,7 @@
             pltpu.SemaphoreType.DMA((2,)),
             pltpu.SemaphoreType.DMA((1,)),
             pltpu.SemaphoreType.DMA((1,)),
-            pltpu.SemaphoreType.DMA((4,)),
+            pltpu.SemaphoreType.DMA((2 * C + 2,)),
         ],
         compiler_params=pltpu.CompilerParams(collective_id=0, has_side_effects=True, vmem_limit_bytes=40000000),
     )(*(pltpu.with_memory_space_constraint(a, pltpu.HBM) for a in (velocity_prev, forcing, reaction, matrix)))

time: 15.7 us -> 15.7 us (level)
  no operation moved by 1% of the time
where the time goes in v8:
time: 15.7 us; the launch traced here: 15.6 us
  Pallas kernels  14.9 us (95%)
  between operations  0.64 us (4%)
    pallas_call x1, Pallas kernels, on_device(): pl.pallas_call(functools.partial(kernel, counts), out_shape=[jax.ShapeDty...  13.5 us
    pallas_call x1, Pallas kernels, on_device(): pl.pallas_call(finish, out_shape=(jax.ShapeDtypeStruct((C, X, Y, Z), jnp....  1.48 us

profile of v8, /device:TPU:0, one launch (start us, length us, event | category | flops | bytes accessed | tf_op | source)
XLA Modules:
  0.0 15.6 jit_solution(16319318552085140300)
XLA Ops:
  0.6 13.5 %shard_map.59 = (f32[3,16,16,32]{3,2,1,0:T(8,128)S(1)}, f32[3,8,16,128]{3,2,1,0:T(8,128)S(1)}, f32[12,24,128]{2,1,0:T(8,128)S(1)}, f32[3,4,32,128]{3,2,1,0:T(8,1...) custom-call(f32[3,8,16,128]{3,2,1,0:T(8,128)} %v_hbm.1, f32[3,8,16,128]{3,2,1,0:T(8,128)} %f_hbm.1, ...), custom_call_target="tpu_custom_call" | custom-call | tf_op jit(solution)/shard_map/pallas_call | solution.py:776
  14.1 1.5 %shard_map.60 = (f32[3,8,16,128]{3,2,1,0:T(8,128)}, f32[3,16,16,32]{3,2,1,0:T(8,128)}) custom-call(f32[3,8,16,128]{3,2,1,0:T(8,128)S(1)} %get-tuple-element.10.base_ref, f32[12,24,128]{2,1,0:T(8,128)S(1)} %get-tuple-element.11.w_ext, f32[3,4,32,128]{3,2,1,0:T(8,128)S(1)} %get-tuple-element.12.q_ext, f32[2,3,32,128]{3,2,1,0:T(8,128)S(1)} %get-tuple-element.13.h_ext, ...), custom_call_target="tpu_custom_call" | custom-call | tf_op jit(solution)/shard_map/pallas_call | solution.py:821

commit v9 on v8

--- a/solution.py
+++ b/solution.py
@@ -305,6 +305,10 @@
                 if t == (tiles_y - 1 if side else 0):
                     first = 6 if side else 0
                     yz_send[side, 2 * i : 2 * i + 2] = packed[first : first + 2]
+    pl.semaphore_wait(barrier, expected)
+    for sides, copy in fine_copies():
+        if len(sides) == 3:
+            pl.when(all_exist(sides, False))(copy.start)
     for number in range(5 * C + 2):
         for side in range(2):
             depth = depth_of(number)
@@ -320,9 +324,9 @@
                     target[3 * c + i : 3 * c + i + 1] = v_ext[c, 3 + x, y : y + 1]
                 target[3 * C + c : 3 * C + c + 1] = f_ext[c, 2 + xs[0], ys[0] : ys[0] + 1]
             target[4 * C : 4 * C + 1] = r_ext[2 + xs[0], ys[0] : ys[0] + 1]
-    pl.semaphore_wait(barrier, expected)
     for sides, copy in fine_copies():
-        pl.when(all_exist(sides, False))(copy.start)
+        if len(sides) < 3:
+            pl.when(all_exist(sides, False))(copy.start)
 
     kept = X // 2
     parts = Y // 8

time: 15.7 us -> 15.8 us (level)
  no operation moved by 1% of the time
where the time goes in v9:
time: 15.8 us; the launch traced here: 15.7 us
  Pallas kernels  15 us (95%)
  between operations  0.64 us (4%)
    pallas_call x1, Pallas kernels, on_device(): pl.pallas_call(functools.partial(kernel, counts), out_shape=[jax.ShapeDty...  13.5 us
    pallas_call x1, Pallas kernels, on_device(): pl.pallas_call(finish, out_shape=(jax.ShapeDtypeStruct((C, X, Y, Z), jnp....  1.48 us

profile of v9, /device:TPU:0, one launch (start us, length us, event | category | flops | bytes accessed | tf_op | source)
XLA Modules:
  0.0 15.7 jit_solution(8007809179075788491)
XLA Ops:
  0.6 13.5 %shard_map.59 = (f32[3,16,16,32]{3,2,1,0:T(8,128)S(1)}, f32[3,8,16,128]{3,2,1,0:T(8,128)S(1)}, f32[12,24,128]{2,1,0:T(8,128)S(1)}, f32[3,4,32,128]{3,2,1,0:T(8,1...) custom-call(f32[3,8,16,128]{3,2,1,0:T(8,128)} %v_hbm.1, f32[3,8,16,128]{3,2,1,0:T(8,128)} %f_hbm.1, ...), custom_call_target="tpu_custom_call" | custom-call | tf_op jit(solution)/shard_map/pallas_call | solution.py:780
  14.2 1.5 %shard_map.60 = (f32[3,8,16,128]{3,2,1,0:T(8,128)}, f32[3,16,16,32]{3,2,1,0:T(8,128)}) custom-call(f32[3,8,16,128]{3,2,1,0:T(8,128)S(1)} %get-tuple-element.10.base_ref, f32[12,24,128]{2,1,0:T(8,128)S(1)} %get-tuple-element.11.w_ext, f32[3,4,32,128]{3,2,1,0:T(8,128)S(1)} %get-tuple-element.12.q_ext, f32[2,3,32,128]{3,2,1,0:T(8,128)S(1)} %get-tuple-element.13.h_ext, ...), custom_call_target="tpu_custom_call" | custom-call | tf_op jit(solution)/shard_map/pallas_call | solution.py:825
